TPU v7x, 32 devices: a whole 2x2x4 slice. The times are simulated.
32 devices in a mesh: role: 4 (over z), dp: 2 (over x), tp: 4 (over y, core).
Axes of the slice: x: 2, y: 2, z: 4, core: 2. Of those that a mesh axis runs over, the one named last changes fastest.
Arguments:
- activations: bfloat16 [2048, 8192], P(('role', 'dp'), 'tp'), may hold values from -6 to 6
- cotangent: bfloat16 [2048, 14336], P(('role', 'dp'), 'tp'), may hold values from -6 to 6
- block_keep: int32 [8], P(('role', 'dp')), may hold values 0 or 1
- input_factor: float32 [64, 8192], P(('role', 'dp'), 'tp'), may hold values from -0.5 to 0.5
- input_mean: float32 [64, 8192], P(('role', 'dp'), 'tp'), may hold values from -6 to 6
- input_square: float32 [64, 8192], P(('role', 'dp'), 'tp'), may hold values from 0.5 to 4
- output_factor: float32 [64, 14336], P(('role', 'dp'), 'tp'), may hold values from -0.3125 to 0.3125
- output_mean: float32 [64, 14336], P(('role', 'dp'), 'tp'), may hold values from -6 to 6
- output_square: float32 [64, 14336], P(('role', 'dp'), 'tp'), may hold values from 0.5 to 4
- frozen_base_rows: bfloat16 [14336, 8192], P(('dp', 'tp')), may hold values from -0.0625 to 0.0625
- prompts: bfloat16 [1024, 8192], P(('role', 'dp', 'tp')), may hold values from -6 to 6
Outputs:
- updated_input: float32 [64, 8192], P(('role', 'dp'), 'tp')
- updated_output: float32 [64, 14336], P(('role', 'dp'), 'tp')
- mean_input: float32 [64, 8192], P(('role', 'dp'), 'tp')
- mean_output: float32 [64, 14336], P(('role', 'dp'), 'tp')
- square_input: float32 [64, 8192], P(('role', 'dp'), 'tp')
- square_output: float32 [64, 14336], P(('role', 'dp'), 'tp')
- merged_weight_rows: bfloat16 [14336, 8192], P(('dp', 'tp'))
- projected: bfloat16 [14336, 1024], P(('dp', 'tp'), 'role')
All inputs are finite; a program needn't handle non-finite values. No bound on the sum of `block_keep` on one device may be relied on, other than what follows from the above.
Results may differ from a plain program's by a relative error of at most 0.006.
Values may be sent and summed in bfloat16 or wider, within the bound.
A program may use at most 128 MiB of HBM per device.

v0:
```python
import functools

import jax
import jax.numpy as jnp
from jax import lax
from jax.experimental import pallas as pl
from jax.experimental.pallas import tpu as pltpu
from jax.sharding import PartitionSpec as P

ROLLOUT_TOKENS = 256


adapter_scale = 2.0
learn_rate = 0.004
beta_one = 0.9
beta_two = 0.95
epsilon = 1e-08
first_fix = 1.0 - 0.9**20
second_fix = 1.0 - 0.95**20


def adam_update(factor, moment, square, gradient):
    moment_new = beta_one * moment + (1.0 - beta_one) * gradient
    square_new = beta_two * square + (1.0 - beta_two) * gradient * gradient
    factor_new = factor - learn_rate * (moment_new / first_fix) / (
        jnp.sqrt(square_new / second_fix) + epsilon
    )
    return (factor_new, moment_new, square_new)


def masked(values, block_keep):
    blocks = block_keep.shape[0]
    reshaped_rows = values.reshape(blocks, values.shape[0] // blocks, values.shape[1])
    weighted = reshaped_rows * block_keep.astype(jnp.float32)[:, None, None]
    return weighted.reshape(values.shape).astype(jnp.bfloat16)


def contract_rows(left, right):
    return lax.dot_general(
        left, right, (((0,), (0,)), ((), ())), preferred_element_type=jnp.float32
    )


def contract_cols(left, right):
    return lax.dot_general(
        left, right, (((1,), (1,)), ((), ())), preferred_element_type=jnp.float32
    )


VMEM = pl.BlockSpec(memory_space=pltpu.VMEM)
MESH = pl.DeviceIdType.MESH


def places():
    return tuple(lax.axis_index(name) for name in ("role", "dp", "tp"))


def sizes():
    return tuple(lax.axis_size(name) for name in ("role", "dp", "tp"))


def enter(peers):
    barrier = pltpu.get_barrier_semaphore()
    for peer in peers:
        pl.semaphore_signal(barrier, inc=1, device_id=peer, device_id_type=MESH)
    pl.semaphore_wait(barrier, len(peers))


def send(source, target, send_sem, recv_sem, peer):
    copy = pltpu.make_async_remote_copy(
        src_ref=source,
        dst_ref=target,
        send_sem=send_sem,
        recv_sem=recv_sem,
        device_id=peer,
        device_id_type=MESH,
    )
    copy.start()
    return copy


def landed(slot, sem):
    pltpu.make_async_copy(slot, slot, sem).wait()


def communicate(kernel, name, outs, scratch, collective_id, args):
    return pl.pallas_call(
        kernel,
        name=name,
        out_shape=outs,
        in_specs=[VMEM] * len(args),
        out_specs=[VMEM] * len(outs),
        scratch_shapes=scratch,
        compiler_params=pltpu.CompilerParams(
            collective_id=collective_id,
            has_side_effects=True,
            vmem_limit_bytes=40 * 1024 * 1024,
        ),
        cost_estimate=pl.CostEstimate(
            flops=10**9, bytes_accessed=10**7, transcendentals=0
        ),
    )(*args)


def dma(*shape):
    return pltpu.SemaphoreType.DMA(shape)


def gather_kernel(count, *refs):
    ins, outs = refs[:count], refs[count : 2 * count]
    own, send_role, recv_role, send_dp, recv_dp = refs[2 * count :]
    role, dp, tp = places()
    roles, dps, _ = sizes()
    role_peers = [(lax.rem(role + k, roles), dp, tp) for k in range(1, roles)]
    dp_peers = [(role, lax.rem(dp + j, dps), tp) for j in range(1, dps)]
    enter(role_peers + dp_peers)
    copies = []
    for i in range(count):
        for k in range(1, roles):
            copies.append(send(ins[i], outs[i].at[dp, role], send_role.at[i, k], recv_role.at[i, k], role_peers[k - 1]))
        for j in range(1, dps):
            copies.append(send(ins[i], outs[i].at[dp, role], send_dp.at[i, j, 0], recv_dp.at[i, j, 0], dp_peers[j - 1]))
        local = pltpu.make_async_copy(ins[i], outs[i].at[dp, role], own.at[i])
        local.start()
    for i in range(count):
        for k in range(1, roles):
            slot = outs[i].at[dp, lax.rem(role + roles - k, roles)]
            landed(slot, recv_role.at[i, k])
            for j in range(1, dps):
                copies.append(send(slot, slot, send_dp.at[i, j, k], recv_dp.at[i, j, k], dp_peers[j - 1]))
    for i in range(count):
        pltpu.make_async_copy(ins[i], outs[i].at[dp, role], own.at[i]).wait()
        for j in range(1, dps):
            for k in range(roles):
                slot = outs[i].at[lax.rem(dp + dps - j, dps), lax.rem(role + roles - k, roles)]
                landed(slot, recv_dp.at[i, j, k])
    for copy in copies:
        copy.wait_send()


def gather_rows(arrays):
    roles, dps, _ = sizes()
    n = len(arrays)
    return communicate(
        functools.partial(gather_kernel, n),
        "gather_rows",
        [jax.ShapeDtypeStruct((dps, roles, *x.shape), x.dtype) for x in arrays],
        [dma(n), dma(n, roles), dma(n, roles), dma(n, dps, roles), dma(n, dps, roles)],
        0,
        arrays,
    )


def features_kernel(count, *refs):
    ins, outs = refs[:count], refs[count : 2 * count]
    slots = refs[2 * count : 3 * count]
    sends, recvs = refs[3 * count :]
    role, dp, tp = places()
    tps = sizes()[2]
    peers = [(role, dp, lax.rem(tp + k, tps)) for k in range(1, tps)]
    enter(peers)
    copies = []
    for i in range(count):
        for k in range(1, tps):
            copies.append(send(ins[i], slots[i].at[k - 1], sends.at[i, k], recvs.at[i, k], peers[k - 1]))
    for i in range(count):
        total = ins[i][...]
        for k in range(1, tps):
            landed(slots[i].at[k - 1], recvs.at[i, k])
            total = total + slots[i][k - 1]
        outs[i][...] = total
    for copy in copies:
        copy.wait_send()


def sum_features(arrays):
    tps = sizes()[2]
    n = len(arrays)
    return communicate(
        functools.partial(features_kernel, n),
        "sum_features",
        [jax.ShapeDtypeStruct(x.shape, x.dtype) for x in arrays],
        [pltpu.VMEM((max(tps - 1, 1), *x.shape), x.dtype) for x in arrays] + [dma(n, tps), dma(n, tps)],
        1,
        arrays,
    )


def tokens_kernel(count, *refs):
    ins, outs = refs[:count], refs[count : 2 * count]
    slots = refs[2 * count : 3 * count]
    sends, recvs = refs[3 * count :]
    role, dp, tp = places()
    roles, dps, _ = sizes()
    offsets = [(j, k) for k in range(roles) for j in range(dps) if (j, k) != (0, 0)]
    offsets.sort(key=lambda o: -min(o[1], roles - o[1]))
    peers = {(j, k): (lax.rem(role + k, roles), lax.rem(dp + j, dps), tp) for j, k in offsets}
    enter(list(peers.values()))
    copies = []
    for i in range(count):
        for j, k in offsets:
            peer = peers[j, k]
            copies.append(send(ins[i].at[peer[1], peer[0]], slots[i].at[j, k], sends.at[i, j, k], recvs.at[i, j, k], peer))
    for i in range(count):
        total = ins[i][dp, role].astype(jnp.float32)
        for j, k in reversed(offsets):
            landed(slots[i].at[j, k], recvs.at[i, j, k])
            total = total + slots[i][j, k].astype(jnp.float32)
        outs[i][...] = total
    for copy in copies:
        copy.wait_send()


def sum_tokens(arrays):
    roles, dps, _ = sizes()
    n = len(arrays)
    return communicate(
        functools.partial(tokens_kernel, n),
        "sum_tokens",
        [jax.ShapeDtypeStruct(x.shape[2:], jnp.float32) for x in arrays],
        [pltpu.VMEM(x.shape, x.dtype) for x in arrays] + [dma(n, dps, roles), dma(n, dps, roles)],
        2,
        arrays,
    )


def spread_kernel(a_ref, b_ref, whole_ref, slice_ref, own, send_b, recv_b, send_role, recv_role, send_dp, recv_dp, send_hi, recv_hi, send_lo, recv_lo):
    role, dp, tp = places()
    roles, dps, tps = sizes()
    half = tps // 2
    devices = roles * dps * tps
    me = (role * dps + dp) * tps + tp

    barrier = pltpu.get_barrier_semaphore()

    @pl.loop(1, devices)
    def _(step):
        other = lax.rem(me + step, devices)
        peer = (other // (dps * tps), lax.rem(other // tps, dps), lax.rem(other, tps))
        pl.semaphore_signal(barrier, inc=1, device_id=peer, device_id_type=MESH)

    pl.semaphore_wait(barrier, devices - 1)

    role_peers = [(lax.rem(role + k, roles), dp, tp) for k in range(1, roles)]
    dp_peers = [(role, lax.rem(dp + j, dps), tp) for j in range(1, dps)]
    hi_peers = [(role, dp, lax.rem(tp + 2 * h, tps)) for h in range(1, half)]
    lo_peer = (role, dp, tp + 1 - 2 * lax.rem(tp, 2))

    home = whole_ref.at[tp, dp, role]
    copies = []
    for k in range(1, roles):
        copies.append(send(a_ref, home, send_role.at[k], recv_role.at[k], role_peers[k - 1]))
    for j in range(1, dps):
        copies.append(send(a_ref, home, send_dp.at[j, 0], recv_dp.at[j, 0], dp_peers[j - 1]))
    local = pltpu.make_async_copy(a_ref, home, own.at[0])
    local.start()

    def b_copy(i, k):
        block = tp * dps + i
        peer = (lax.rem(role + k, roles), block // tps, lax.rem(block, tps))
        place = slice_ref.at[dp, role]
        remote = pltpu.make_async_remote_copy(
            src_ref=b_ref.at[i], dst_ref=place, send_sem=send_b.at[i, k], recv_sem=recv_b.at[dp, role],
            device_id=peer, device_id_type=MESH,
        )
        if k > 0:
            return None, remote, None
        here = (block // tps == dp) & (lax.rem(block, tps) == tp)
        return here, remote, pltpu.make_async_copy(b_ref.at[i], place, recv_b.at[dp, role])

    for k in range(roles):
        for i in range(dps):
            here, remote, beside = b_copy(i, k)
            if here is None:
                remote.start()
            else:
                pl.when(here)(beside.start)
                pl.when(jnp.logical_not(here))(remote.start)

    for k in range(1, roles):
        slot = whole_ref.at[tp, dp, lax.rem(role + roles - k, roles)]
        landed(slot, recv_role.at[k])
        for j in range(1, dps):
            copies.append(send(slot, slot, send_dp.at[j, k], recv_dp.at[j, k], dp_peers[j - 1]))
    local.wait()
    for j in range(dps):
        from_dp = lax.rem(dp + dps - j, dps)
        if j > 0:
            for k in range(roles):
                landed(whole_ref.at[tp, from_dp, lax.rem(role + roles - k, roles)], recv_dp.at[j, k])
        group = whole_ref.at[tp, from_dp]
        for h in range(1, half):
            copies.append(send(group, group, send_hi.at[h, j], recv_hi.at[h, j], hi_peers[h - 1]))
        copies.append(send(group, group, send_lo.at[0, j], recv_lo.at[0, j], lo_peer))
    for j in range(dps):
        from_dp = lax.rem(dp + dps - j, dps)
        for h in range(1, half):
            group = whole_ref.at[lax.rem(tp + tps - 2 * h, tps), from_dp]
            landed(group, recv_hi.at[h, j])
            copies.append(send(group, group, send_lo.at[h, j], recv_lo.at[h, j], lo_peer))
    other = lo_peer[2]
    for j in range(dps):
        from_dp = lax.rem(dp + dps - j, dps)
        for h in range(half):
            landed(whole_ref.at[lax.rem(other + tps - 2 * h, tps), from_dp], recv_lo.at[h, j])
    for d in range(dps):
        for r in range(roles):
            landed(slice_ref.at[d, r], recv_b.at[d, r])
    for k in range(roles):
        for i in range(dps):
            here, remote, _ = b_copy(i, k)
            if here is None:
                remote.wait_send()
            else:
                pl.when(jnp.logical_not(here))(remote.wait_send)
    for copy in copies:
        copy.wait_send()


def spread(a, b):
    roles, dps, tps = sizes()
    half = max(tps // 2, 1)
    return communicate(
        spread_kernel,
        "spread",
        [
            jax.ShapeDtypeStruct((tps, dps, roles, *a.shape), a.dtype),
            jax.ShapeDtypeStruct((dps, roles, *b.shape[1:]), b.dtype),
        ],
        [
            dma(1), dma(dps, roles), dma(dps, roles), dma(roles), dma(roles),
            dma(dps, roles), dma(dps, roles), dma(half, dps), dma(half, dps), dma(half, dps), dma(half, dps),
        ],
        3,
        [a, b],
    )


def merge_kernel(base_ref, b_ref, a_ref, prompts_ref, merged_ref, projected_ref):
    shards, _, width = a_ref.shape
    total = jnp.zeros(projected_ref.shape, jnp.float32)
    for shard in range(shards):
        columns = pl.ds(shard * width, width)
        delta = jnp.dot(b_ref[...], a_ref[shard], preferred_element_type=jnp.float32)
        merged = (base_ref[:, columns].astype(jnp.float32) + adapter_scale * delta).astype(jnp.bfloat16)
        merged_ref[:, columns] = merged
        total = total + contract_cols(merged, prompts_ref[:, columns])
    projected_ref[...] = total.astype(projected_ref.dtype)


def merge(base, b, a, prompts):
    rows, width = base.shape
    tile = max(t for t in range(16, 257, 16) if rows % t == 0)
    count = prompts.shape[0]
    return pl.pallas_call(
        merge_kernel,
        name="merge",
        grid=(rows // tile,),
        out_shape=[
            jax.ShapeDtypeStruct(base.shape, base.dtype),
            jax.ShapeDtypeStruct((rows, count), jnp.bfloat16),
        ],
        in_specs=[
            pl.BlockSpec((tile, width), lambda i: (i, 0)),
            pl.BlockSpec((tile, b.shape[1]), lambda i: (i, 0)),
            VMEM,
            VMEM,
        ],
        out_specs=[
            pl.BlockSpec((tile, width), lambda i: (i, 0)),
            pl.BlockSpec((tile, count), lambda i: (i, 0)),
        ],
        compiler_params=pltpu.CompilerParams(vmem_limit_bytes=56 * 1024 * 1024),
        cost_estimate=pl.CostEstimate(
            flops=2 * rows * width * (count + b.shape[1]), bytes_accessed=4 * rows * width, transcendentals=0
        ),
    )(base, b, a, prompts)


def body(
    activations,
    cotangent,
    block_keep,
    input_factor,
    input_mean,
    input_square,
    output_factor,
    output_mean,
    output_square,
    frozen_base_rows,
    prompts,
):
    roles, dps, tps = sizes()
    rows = input_factor.shape[0]
    rank = roles * dps * rows
    group_prompts = lax.all_gather(prompts, ("dp", "tp"), axis=0, tiled=True)
    input_rows, output_rows = gather_rows(
        [input_factor.astype(jnp.bfloat16), output_factor.astype(jnp.bfloat16)]
    )
    low_input = contract_cols(activations, input_rows.reshape(rank, -1))
    low_grad = contract_cols(cotangent, output_rows.reshape(rank, -1))
    low_input, low_grad = sum_features([low_input, low_grad])
    input_kept = masked(low_input, block_keep)
    grad_kept = masked(low_grad, block_keep)
    input_part = contract_rows(grad_kept, activations).astype(jnp.bfloat16)
    output_part = contract_rows(input_kept, cotangent).astype(jnp.bfloat16)
    input_sum, output_sum = sum_tokens(
        [part.reshape(dps, roles, rows, -1) for part in (input_part, output_part)]
    )
    adapter_factor_scale = adapter_scale / ROLLOUT_TOKENS
    input_new, input_moment, input_second = adam_update(
        input_factor, input_mean, input_square, input_sum * adapter_factor_scale
    )
    output_new, output_moment, output_second = adam_update(
        output_factor, output_mean, output_square, output_sum * adapter_factor_scale
    )
    input_send = input_new.astype(jnp.bfloat16)
    output_send = output_new.astype(jnp.bfloat16).reshape(rows, dps, -1).swapaxes(0, 1)
    input_whole, output_slice = spread(input_send, output_send)
    merged_weight_rows, projected = merge(
        frozen_base_rows,
        output_slice.reshape(rank, -1).T,
        input_whole.reshape(tps, rank, -1),
        group_prompts,
    )
    return (
        input_new,
        output_new,
        input_moment,
        output_moment,
        input_second,
        output_second,
        merged_weight_rows,
        projected,
    )


def solution(mesh):
    placed = (
        P(("role", "dp"), "tp"),
        P(("role", "dp"), "tp"),
        P(("role", "dp")),
        P(("role", "dp"), "tp"),
        P(("role", "dp"), "tp"),
        P(("role", "dp"), "tp"),
        P(("role", "dp"), "tp"),
        P(("role", "dp"), "tp"),
        P(("role", "dp"), "tp"),
        P(("dp", "tp"), None),
        P(("role", "dp", "tp"), None),
    )
    return jax.shard_map(
        body,
        mesh=mesh,
        in_specs=placed,
        out_specs=(
            P(("role", "dp"), "tp"),
            P(("role", "dp"), "tp"),
            P(("role", "dp"), "tp"),
            P(("role", "dp"), "tp"),
            P(("role", "dp"), "tp"),
            P(("role", "dp"), "tp"),
            P(("dp", "tp"), None),
            P(("dp", "tp"), "role"),
        ),
        check_vma=False,
    )
```

profile of v0, /device:TPU:3, one launch (start us, length us, event | category | flops | bytes accessed | tf_op | source)
XLA Modules:
  0.0 133.9 jit_solution(15018102060724141182)
XLA Ops:
  7.2 0.0 copy-start
  7.2 0.0 all-gather.2.cloned.1.call-start
  7.2 0.7 all-gather.2.cloned.1.call-update
  8.6 0.8 convert_element_type.28.refs_0_
  9.4 0.9 convert_element_type.29.refs_1_
  10.3 16.9 %gather_rows.1 = (bf16[2,4,8,2048]{3,2,1,0:T(8,128)(2,1)S(1)}, bf16[2,4,8,3584]{3,2,1,0:T(8,128)(2,1)S(1)}) custom-call(bf16[8,2048]{1,0:T(8,128)(2,1)S(1)} %convert_element_type.28.refs_0_, bf16[8,3584]{1,0:T(8,128)(2,1)S(1)} %convert_element_type.29.refs_1_), custom_call_target="tpu_custom_call" | custom-call | flops 1000000000 | bytes 10000000 | tf_op jit(solution)/shard_map/gather_rows/pallas_call | solution.py:87
  27.2 0.4 convolution_bitcast_fusion.1.refs_0_
  27.7 0.6 convolution_bitcast_fusion.refs_1_
  28.3 25.4 %sum_features.1 = (f32[256,64]{1,0:T(8,128)S(1)}, f32[256,64]{1,0:T(8,128)S(1)}) custom-call(f32[256,64]{1,0:T(8,128)S(1)} %convolution_bitcast_fusion.1.refs_0_, f32[256,64]{1,0:T(8,128)S(1)} %convolution_bitcast_fusion.refs_1_), custom_call_target="tpu_custom_call" | custom-call | flops 1000000000 | bytes 10000000 | tf_op jit(solution)/shard_map/sum_features/pallas_call | solution.py:87
  53.7 0.3 convolution_convert_fusion.1
  54.1 0.5 convolution_convert_fusion
  54.5 0.0 copy-start.5
  54.5 0.0 copy-start.8
  54.6 0.0 copy-start.9
  54.6 0.0 copy-start.4
  54.6 0.0 copy-start.6
  54.6 0.0 copy-start.7
  54.6 18.0 %sum_tokens.1 = (f32[8,2048]{1,0:T(8,128)S(1)}, f32[8,3584]{1,0:T(8,128)S(1)}) custom-call(bf16[2,4,8,2048]{3,2,1,0:T(8,128)(2,1)S(1)} %bitcast.24, bf16[2,4,8,3584]{3,2,1,0:T(8,128)(2,1)S(1)} %bitcast.23), custom_call_target="tpu_custom_call" | custom-call | flops 1000000000 | bytes 10000000 | tf_op jit(solution)/shard_map/sum_tokens/pallas_call | solution.py:87
  72.6 0.7 fusion.3
  73.3 0.8 fusion.2
  74.1 22.4 %spread.1 = (bf16[4,2,4,8,2048]{4,3,2,1,0:T(8,128)(2,1)S(1)}, bf16[2,4,8,1792]{3,2,1,0:T(8,128)(2,1)S(1)}) custom-call(bf16[8,2048]{1,0:T(8,128)(2,1)S(1)} %get-tuple-element.32.a_ref, bf16[2,8,1792]{2,1,0:T(8,128)(2,1)S(1)} %bitcast.27), custom_call_target="tpu_custom_call" | custom-call | flops 1000000000 | bytes 10000000 | tf_op jit(solution)/shard_map/spread/pallas_call | solution.py:87
  96.6 1.0 copy-done.2
  97.5 1.0 copy.24
  98.5 28.5 %merge.1 = (bf16[1792,8192]{1,0:T(8,128)(2,1)}, bf16[1792,256]{1,0:T(8,128)(2,1)}) custom-call(bf16[1792,8192]{1,0:T(8,128)(2,1)} %base_ref.1, bf16[1792,64]{1,0:T(8,128)(2,1)} %bitcast.28, bf16[4,64,2048]{2,1,0:T(8,128)(2,1)} %bitcast.21, bf16[256,8192]{1,0:T(8,128)(2,1)} %all-gather.2.cloned.1.call-done.prompts_ref), custom_call_target="tpu_custom_call" | custom-call | flops 9395240960 | bytes 58720256 | tf_op jit(solution)/shard_map/merge/pallas_call | solution.py:355
  (13 shorter events, 0.0 us)
Async XLA Ops:
  7.2 20.5 %copy-start = (bf16[256,3584]{1,0:T(8,128)(2,1)S(1)}, bf16[256,3584]{1,0:T(8,128)(2,1)}, u32[]{:S(2)}) copy-start(bf16[256,3584]{1,0:T(8,128)(2,1)} %param.12) | copy-start | bytes 5505028
  7.2 91.4 %all-gather.2.cloned.1.call-start = ((), (), s32[]{:S(2)}) async-start(), calls=%async_computation | async-start | bytes 4718592 | tf_op jit(solution)/shard_map/all_gather | solution.py:396
  10.3 16.9 %copy-start.3 = (bf16[256,2048]{1,0:T(8,128)(2,1)S(1)}, bf16[256,2048]{1,0:T(8,128)(2,1)}, u32[]{:S(2)}) copy-start(bf16[256,2048]{1,0:T(8,128)(2,1)} %param.11) | copy-start | bytes 3145732
  54.5 18.1 %copy-start.5 = (f32[8,2048]{1,0:T(8,128)S(1)}, f32[8,2048]{1,0:T(8,128)}, u32[]{:S(2)}) copy-start(f32[8,2048]{1,0:T(8,128)} %param.14) | copy-start | bytes 196612
  54.5 18.1 %copy-start.8 = (f32[8,2048]{1,0:T(8,128)S(1)}, f32[8,2048]{1,0:T(8,128)}, u32[]{:S(2)}) copy-start(f32[8,2048]{1,0:T(8,128)} %param.15) | copy-start | bytes 196612
  54.6 18.1 %copy-start.9 = (f32[8,2048]{1,0:T(8,128)S(1)}, f32[8,2048]{1,0:T(8,128)}, u32[]{:S(2)}) copy-start(f32[8,2048]{1,0:T(8,128)} %param.16) | copy-start | bytes 196612
  54.6 18.8 %copy-start.4 = (f32[8,3584]{1,0:T(8,128)S(1)}, f32[8,3584]{1,0:T(8,128)}, u32[]{:S(2)}) copy-start(f32[8,3584]{1,0:T(8,128)} %param.17) | copy-start | bytes 344068
  54.6 18.8 %copy-start.6 = (f32[8,3584]{1,0:T(8,128)S(1)}, f32[8,3584]{1,0:T(8,128)}, u32[]{:S(2)}) copy-start(f32[8,3584]{1,0:T(8,128)} %param.18) | copy-start | bytes 344068
  54.6 18.8 %copy-start.7 = (f32[8,3584]{1,0:T(8,128)S(1)}, f32[8,3584]{1,0:T(8,128)}, u32[]{:S(2)}) copy-start(f32[8,3584]{1,0:T(8,128)} %param.19) | copy-start | bytes 344068
  96.6 1.0 copy-start.2
  98.5 28.5 %copy-start.1 = (bf16[256,3584]{1,0:T(8,128)(2,1)S(1)}, bf16[256,3584]{1,0:T(8,128)(2,1)}, u32[]{:S(2)}) copy-start(bf16[256,3584]{1,0:T(8,128)(2,1)} %param.12) | copy-start | bytes 5505028
Sparse Core Ops, SparseCore 0:
  9.9 48.8 all-gather.1
where the time goes:
time: 134 us
  Pallas kernels  111 us (83%)
  between operations  14.8 us (11%)
  other arithmetic  3.21 us (2%)
  local copies, waits for them, and re-layouts  2.03 us (2%)
  matrix products  1.82 us (1%)
    pallas_call x4, Pallas kernels, communicate(): pl.pallas_call(kernel, name=name, out_shape=outs, in_specs=[VMEM] * len(a...  82.8 us
    pallas_call x1, Pallas kernels, merge(): pl.pallas_call(merge_kernel, name='merge', grid=(rows // tile,), out_shap...  28.5 us
  transfers between devices with their start and end apart: 1, of which 0 were waited for; matrix products, arithmetic and copies ran while one was open for 5% of the time, Pallas kernels for 62%

commit v1 on v0

--- a/solution.py
+++ b/solution.py
@@ -435,6 +435,407 @@
     )
 
 
+HBM = pl.BlockSpec(memory_space=pltpu.HBM)
+SMEM = pl.BlockSpec(memory_space=pltpu.SMEM)
+PARTS = 4
+
+
+class Wires:
+    def __init__(self, sends, recvs):
+        self.sends, self.recvs, self.copies, self.used = sends, recvs, [], 0
+
+    def send(self, source, target, peer):
+        place = self.used
+        self.used += 1
+        self.copies.append(send(source, target, self.sends.at[place], self.recvs.at[place], peer))
+        return place
+
+    def landed(self, slot, place):
+        landed(slot, self.recvs.at[place])
+
+    def drain(self):
+        for copy in self.copies:
+            copy.wait_send()
+
+
+def far_first(count):
+    return sorted(range(1, count), key=lambda k: -min(k, count - k))
+
+
+def step_kernel(
+    act_hbm, cot_hbm, keep_ref, a_hbm, am_hbm, av_hbm, b_hbm, bm_hbm, bv_hbm, prompts_hbm,
+    a_new, a_mom, a_sec, b_new, b_mom, b_sec, whole, piece, group,
+    act, cot, a, am, av, b, bm, bv, fa, fb, la, lb, ra, rb, pa, pb, xa, xb, sa, sb, za, zb, oa, ob, b_send,
+    local, sends, recvs, b_sends, b_recvs,
+):
+    role, dp, tp = places()
+    roles, dps, tps = sizes()
+    half = tps // 2
+    devices = roles * dps * tps
+    me = (role * dps + dp) * tps + tp
+    scale = adapter_scale / ROLLOUT_TOKENS
+    bf16, f32 = jnp.bfloat16, jnp.float32
+    wires = Wires(sends, recvs)
+
+    loads = {}
+    pairs = [("a", a_hbm, a), ("b", b_hbm, b), ("act", act_hbm, act), ("cot", cot_hbm, cot), ("am", am_hbm, am),
+             ("av", av_hbm, av), ("bm", bm_hbm, bm), ("bv", bv_hbm, bv), ("own", prompts_hbm, group.at[dp, tp])]
+    for i, (name, source, target) in enumerate(pairs):
+        loads[name] = pltpu.make_async_copy(source, target, local.at[i])
+        loads[name].start()
+
+    barrier = pltpu.get_barrier_semaphore()
+
+    @pl.loop(1, devices)
+    def _(step):
+        other = lax.rem(me + step, devices)
+        peer = (other // (dps * tps), lax.rem(other // tps, dps), lax.rem(other, tps))
+        pl.semaphore_signal(barrier, inc=1, device_id=peer, device_id_type=MESH)
+
+    loads["a"].wait()
+    fa[dp, role] = a[...].astype(bf16)
+    loads["b"].wait()
+    fb[dp, role] = b[...].astype(bf16)
+    pl.semaphore_wait(barrier, devices - 1)
+
+    role_of = lambda k: lax.rem(role + k, roles)
+    role_back = lambda k: lax.rem(role + roles - k, roles)
+    dp_of = lambda j: lax.rem(dp + j, dps)
+    dp_back = lambda j: lax.rem(dp + dps - j, dps)
+    tp_back = lambda k: lax.rem(tp + tps - k, tps)
+    role_peer = lambda k: (role_of(k), dp, tp)
+    dp_peer = lambda j: (role, dp_of(j), tp)
+    tp_peer = lambda k: (role, dp, lax.rem(tp + k, tps))
+    other = tp + 1 - 2 * lax.rem(tp, 2)
+    lo_peer = (role, dp, other)
+    far = far_first(roles)
+    near = far[::-1]
+
+    def gather_start(ref):
+        home = ref.at[dp, role]
+        to_role = {k: wires.send(home, home, role_peer(k)) for k in near}
+        to_dp = {(j, 0): wires.send(home, home, dp_peer(j)) for j in range(1, dps)}
+        return to_role, to_dp
+
+    def gather_forward(ref, to_role, to_dp):
+        for k in near:
+            slot = ref.at[dp, role_back(k)]
+            wires.landed(slot, to_role[k])
+            for j in range(1, dps):
+                to_dp[j, k] = wires.send(slot, slot, dp_peer(j))
+
+    def gather_finish(ref, to_dp):
+        for (j, k), place in to_dp.items():
+            wires.landed(ref.at[dp_back(j), role_back(k)], place)
+
+    width = prompts_hbm.shape[1] // PARTS
+    part = lambda ref, c: ref.at[:, pl.ds(c * width, width)]
+    spot = lambda d, t, c: group.at[d, t, :, pl.ds(c * width, width)]
+    via_dp = PARTS // 2
+    hi_own, lo_own, dp_own, hi_far, dp_far, lo_ids = {}, {}, {}, {}, {}, {}
+
+    def prompts_first():
+        for c in range(PARTS):
+            for h in range(1, half):
+                hi_own[h, c] = wires.send(part(prompts_hbm, c), spot(dp, tp, c), tp_peer(2 * h))
+            lo_own[c] = wires.send(part(prompts_hbm, c), spot(dp, tp, c), lo_peer)
+
+    def prompts_across(parts):
+        for c in parts:
+            for j in range(1, dps):
+                dp_own[j, c] = wires.send(part(prompts_hbm, c), spot(dp, tp, c), dp_peer(j))
+
+    def prompts_hi_landed(parts):
+        for c in parts:
+            for h in range(1, half):
+                slot = spot(dp, tp_back(2 * h), c)
+                wires.landed(slot, hi_own[h, c])
+                lo_ids[0, h, c] = wires.send(slot, slot, lo_peer)
+                if c < via_dp:
+                    for j in range(1, dps):
+                        dp_far[j, h, c] = wires.send(slot, slot, dp_peer(j))
+
+    def prompts_dp_landed(parts):
+        for c in parts:
+            for j in range(1, dps):
+                slot = spot(dp_back(j), tp, c)
+                wires.landed(slot, dp_own[j, c])
+                lo_ids[j, 0, c] = wires.send(slot, slot, lo_peer)
+                if c >= via_dp:
+                    for h in range(1, half):
+                        hi_far[j, h, c] = wires.send(slot, slot, tp_peer(2 * h))
+
+    def prompts_far_landed():
+        for c in range(PARTS):
+            for j in range(1, dps):
+                for h in range(1, half):
+                    slot = spot(dp_back(j), tp_back(2 * h), c)
+                    wires.landed(slot, dp_far[j, h, c] if c < via_dp else hi_far[j, h, c])
+                    lo_ids[j, h, c] = wires.send(slot, slot, lo_peer)
+
+    def prompts_finish():
+        for c, place in lo_own.items():
+            wires.landed(spot(dp, other, c), place)
+        for (j, h, c), place in lo_ids.items():
+            wires.landed(spot(dp_back(j), lax.rem(other + tps - 2 * h, tps), c), place)
+
+    a_role, a_dp = gather_start(fa)
+    b_role, b_dp = gather_start(fb)
+    prompts_first()
+    gather_forward(fa, a_role, a_dp)
+    gather_forward(fb, b_role, b_dp)
+    prompts_across(range(via_dp))
+
+    def low_start(ref, to_dp, tokens, name, low):
+        gather_finish(ref, to_dp)
+        loads[name].wait()
+        rows = ref[...].reshape(-1, ref.shape[-1])
+        low[...] = contract_cols(rows, tokens[...]).astype(bf16)
+        return [wires.send(low, (ra if low is la else rb).at[k - 1], tp_peer(k)) for k in range(1, tps)]
+
+    def low_finish(low, slots, ids):
+        total = low[...].astype(f32)
+        for k in range(1, tps):
+            wires.landed(slots.at[k - 1], ids[k - 1])
+            total = total + slots[k - 1].astype(f32)
+        return (total * keep_ref[0].astype(f32)).astype(bf16)
+
+    a_low = low_start(fa, a_dp, act, "act", la)
+    b_low = low_start(fb, b_dp, cot, "cot", lb)
+
+    order = far + [0]
+
+    def reduce_start(ref, kept, tokens, x_slots):
+        grads = jnp.dot(kept, tokens[...], preferred_element_type=f32).astype(bf16)
+        ref[...] = grads.reshape(ref.shape)
+        ids = {}
+        for k in order:
+            for j in range(1, dps):
+                ids[j, k] = wires.send(ref.at[dp_of(j), role_of(k)], x_slots.at[j - 1, role_of(k)], dp_peer(j))
+        return ids
+
+    def reduce_middle(ref, x_slots, x_ids, s_slots, z_slots, own):
+        ids = {}
+        for k in order:
+            total = ref[dp, role_of(k)].astype(f32)
+            for j in range(1, dps):
+                wires.landed(x_slots.at[j - 1, role], x_ids[j, k]) if k == 0 else wires.landed(
+                    x_slots.at[j - 1, role_of(k)], x_ids[j, k])
+                total = total + x_slots[j - 1, role_of(k)].astype(f32)
+            if k == 0:
+                own[...] = total
+            else:
+                s_slots[k - 1] = total.astype(bf16)
+                ids[k] = wires.send(s_slots.at[k - 1], z_slots.at[k - 1], role_peer(k))
+        return ids
+
+    def reduce_finish(own, z_slots, ids):
+        total = own[...]
+        for k in order[:-1]:
+            wires.landed(z_slots.at[k - 1], ids[k])
+            total = total + z_slots[k - 1].astype(f32)
+        return total * scale
+
+    kept_in = low_finish(la, ra, a_low)
+    xb_ids = reduce_start(pb, kept_in, cot, xb)
+    kept_grad = low_finish(lb, rb, b_low)
+    xa_ids = reduce_start(pa, kept_grad, act, xa)
+    prompts_hi_landed(range(PARTS))
+    zb_ids = reduce_middle(pb, xb, xb_ids, sb, zb, ob)
+    za_ids = reduce_middle(pa, xa, xa_ids, sa, za, oa)
+    prompts_across(range(via_dp, PARTS))
+    prompts_dp_landed(range(via_dp))
+
+    for name in ("am", "av", "bm", "bv"):
+        loads[name].wait()
+
+    fresh, mom, sec = adam_update(b[...], bm[...], bv[...], reduce_finish(ob, zb, zb_ids))
+    b_new[...], b_mom[...], b_sec[...] = fresh, mom, sec
+    columns = fresh.shape[1] // dps
+    for i in range(dps):
+        b_send[i] = fresh[:, i * columns : (i + 1) * columns].astype(bf16)
+
+    def b_copy(i, k):
+        block = tp * dps + i
+        peer = (role_of(k), block // tps, lax.rem(block, tps))
+        place = piece.at[dp, role]
+        remote = pltpu.make_async_remote_copy(
+            src_ref=b_send.at[i], dst_ref=place, send_sem=b_sends.at[i, k], recv_sem=b_recvs.at[dp, role],
+            device_id=peer, device_id_type=MESH,
+        )
+        if k > 0:
+            return None, remote, None
+        here = (block // tps == dp) & (lax.rem(block, tps) == tp)
+        return here, remote, pltpu.make_async_copy(b_send.at[i], place, b_recvs.at[dp, role])
+
+    for k in far + [0]:
+        for i in range(dps):
+            here, remote, beside = b_copy(i, k)
+            if here is None:
+                remote.start()
+            else:
+                pl.when(here)(beside.start)
+                pl.when(jnp.logical_not(here))(remote.start)
+
+    fresh, mom, sec = adam_update(a[...], am[...], av[...], reduce_finish(oa, za, za_ids))
+    whole[tp, dp, role] = fresh.astype(bf16)
+    a_new[...], a_mom[...], a_sec[...] = fresh, mom, sec
+    mine = whole.at[tp]
+    a_role, a_dp = gather_start(mine)
+    gather_forward(mine, a_role, a_dp)
+    hi_ids, lo_a = {}, {}
+    for j in range(dps):
+        if j > 0:
+            for k in range(roles):
+                wires.landed(mine.at[dp_back(j), role_back(k)], a_dp[j, k])
+        slot = mine.at[dp_back(j)]
+        for h in range(1, half):
+            hi_ids[h, j] = wires.send(slot, slot, tp_peer(2 * h))
+        lo_a[0, j] = wires.send(slot, slot, lo_peer)
+    prompts_dp_landed(range(via_dp, PARTS))
+    prompts_far_landed()
+    for j in range(dps):
+        for h in range(1, half):
+            slot = whole.at[tp_back(2 * h), dp_back(j)]
+            wires.landed(slot, hi_ids[h, j])
+            lo_a[h, j] = wires.send(slot, slot, lo_peer)
+    for (h, j), place in lo_a.items():
+        wires.landed(whole.at[lax.rem(other + tps - 2 * h, tps), dp_back(j)], place)
+    for d in range(dps):
+        for r in range(roles):
+            landed(piece.at[d, r], b_recvs.at[d, r])
+    prompts_finish()
+    loads["own"].wait()
+    for k in range(roles):
+        for i in range(dps):
+            here, remote, _ = b_copy(i, k)
+            if here is None:
+                remote.wait_send()
+            else:
+                pl.when(jnp.logical_not(here))(remote.wait_send)
+    wires.drain()
+
+
+def step(activations, cotangent, block_keep, a, am, av, b, bm, bv, prompts):
+    roles, dps, tps = sizes()
+    tokens, a_width = activations.shape
+    b_width = cotangent.shape[1]
+    rows = a.shape[0]
+    rank = roles * dps * rows
+    bf16, f32 = jnp.bfloat16, jnp.float32
+    vmem = pltpu.VMEM
+    args = [activations, cotangent, block_keep, a, am, av, b, bm, bv, prompts]
+    outs = [jax.ShapeDtypeStruct(x.shape, f32) for x in (a, a, a, b, b, b)] + [
+        jax.ShapeDtypeStruct((tps, dps, roles, rows, a_width), bf16),
+        jax.ShapeDtypeStruct((dps, roles, rows, b_width // dps), bf16),
+        jax.ShapeDtypeStruct((dps, tps, *prompts.shape), bf16),
+    ]
+    wide = lambda *lead: [vmem((*lead, rows, w), bf16) for w in (a_width, b_width)]
+    return pl.pallas_call(
+        step_kernel,
+        name="step",
+        out_shape=outs,
+        in_specs=[HBM, HBM, SMEM] + [HBM] * 7,
+        out_specs=[VMEM] * len(outs),
+        scratch_shapes=[vmem(activations.shape, bf16), vmem(cotangent.shape, bf16)]
+        + [vmem(a.shape, f32)] * 3
+        + [vmem(b.shape, f32)] * 3
+        + wide(dps, roles)
+        + [vmem((rank, tokens), bf16)] * 2
+        + [vmem((tps - 1, rank, tokens), bf16)] * 2
+        + wide(dps, roles)
+        + wide(dps - 1, roles)
+        + wide(roles - 1)
+        + wide(roles - 1)
+        + [vmem(a.shape, f32), vmem(b.shape, f32), vmem((dps, rows, b_width // dps), bf16)]
+        + [dma(9), dma(160), dma(160), dma(dps, roles), dma(dps, roles)],
+        compiler_params=pltpu.CompilerParams(
+            collective_id=0, has_side_effects=True, vmem_limit_bytes=40 * 1024 * 1024
+        ),
+        cost_estimate=pl.CostEstimate(flops=10**9, bytes_accessed=10**7, transcendentals=0),
+    )(*args)
+
+
+def finish_kernel(base_ref, b_ref, a_ref, prompts_ref, *refs):
+    small, (merged_ref, projected_ref), copies = refs[:6], refs[6:8], refs[8:]
+
+    @pl.when(pl.program_id(0) == 0)
+    def _():
+        for source, target in zip(small, copies):
+            target[...] = source[...]
+
+    shards, _, width = a_ref.shape
+    total = jnp.zeros(projected_ref.shape, jnp.float32)
+    for shard in range(shards):
+        columns = pl.ds(shard * width, width)
+        delta = contract_rows(b_ref[...], a_ref[shard])
+        merged = (base_ref[:, columns].astype(jnp.float32) + adapter_scale * delta).astype(jnp.bfloat16)
+        merged_ref[:, columns] = merged
+        total = total + contract_cols(merged, prompts_ref[:, columns])
+    projected_ref[...] = total.astype(projected_ref.dtype)
+
+
+def finish(base, b, a, prompts, small):
+    rows, width = base.shape
+    tile = max(t for t in range(128, 257, 128) if rows % t == 0)
+    count = prompts.shape[0]
+    return pl.pallas_call(
+        finish_kernel,
+        name="finish",
+        grid=(rows // tile,),
+        out_shape=[
+            jax.ShapeDtypeStruct(base.shape, base.dtype),
+            jax.ShapeDtypeStruct((rows, count), jnp.bfloat16),
+        ]
+        + [jax.ShapeDtypeStruct(x.shape, x.dtype) for x in small],
+        in_specs=[
+            pl.BlockSpec((tile, width), lambda i: (i, 0)),
+            pl.BlockSpec((b.shape[0], tile), lambda i: (0, i)),
+        ]
+        + [VMEM] * (2 + len(small)),
+        out_specs=[
+            pl.BlockSpec((tile, width), lambda i: (i, 0)),
+            pl.BlockSpec((tile, count), lambda i: (i, 0)),
+        ]
+        + [VMEM] * len(small),
+        compiler_params=pltpu.CompilerParams(vmem_limit_bytes=40 * 1024 * 1024),
+        cost_estimate=pl.CostEstimate(
+            flops=2 * rows * width * (count + b.shape[0]), bytes_accessed=4 * rows * width, transcendentals=0
+        ),
+    )(base, b, a, prompts, *small)
+
+
+def fused_body(
+    activations, cotangent, block_keep, input_factor, input_mean, input_square,
+    output_factor, output_mean, output_square, frozen_base_rows, prompts,
+):
+    roles, dps, tps = sizes()
+    rank = roles * dps * input_factor.shape[0]
+    *small, whole, piece, group = step(
+        activations, cotangent, block_keep, input_factor, input_mean, input_square,
+        output_factor, output_mean, output_square, prompts,
+    )
+    merged, projected, *copies = finish(
+        frozen_base_rows,
+        piece.reshape(rank, -1),
+        whole.reshape(tps, rank, -1),
+        group.reshape(-1, prompts.shape[1]),
+        small,
+    )
+    a_new, a_mom, a_sec, b_new, b_mom, b_sec = copies
+    return a_new, b_new, a_mom, b_mom, a_sec, b_sec, merged, projected
+
+
+def chosen_body(*args):
+    roles, dps, tps = sizes()
+    blocks, rows = args[2].shape[0], args[3].shape[0]
+    base_rows = args[9].shape[0]
+    fits = rows % 8 == 0 and args[10].shape[0] % 8 == 0 and base_rows % 128 == 0
+    if blocks == 1 and min(roles, dps) > 1 and tps % 2 == 0 and fits:
+        return fused_body(*args)
+    return body(*args)
+
+
 def solution(mesh):
     placed = (
         P(("role", "dp"), "tp"),
@@ -450,7 +851,7 @@
         P(("role", "dp", "tp"), None),
     )
     return jax.shard_map(
-        body,
+        chosen_body,
         mesh=mesh,
         in_specs=placed,
         out_specs=(

time: 134 us -> 101 us (0.75)
  Pallas kernels: 111 us -> 90.6 us
  between operations: 14.8 us -> 1.31 us
  local copies, waits for them, and re-layouts: 2.03 us -> 8.97 us
  other arithmetic: 3.21 us -> 0 us
  matrix products: 1.82 us -> 0 us
    pallas_call x5 -> x2, Pallas kernels: 111 us -> 90.6 us  [the longest x1 65.4 us: step(): pl.pallas_call(step_kernel, name='step', out_shape=outs, in_specs=[HBM, H...]
    unnamed x20 -> x18, local copies, waits for them, and re-layouts: 1.02 us -> 8.97 us
    convert_element_type x4 -> x0, other arithmetic: 3.21 us -> none  [the longest x1 0.91 us: body(): output_factor.astype(jnp.bfloat16)]
    dot_general x4 -> x0, matrix products: 1.82 us -> none  [the longest x2 1.03 us: contract_cols(): lax.dot_general(left, right, (((1,), (1,)), ((), ())), preferred_element_...]
  transfers between devices with their start and end apart: 1 -> 0, of which waited for: 0 -> 0; matrix products, arithmetic and copies ran while one was open for 5% -> 0% of each run, Pallas kernels for 62% -> 0%
where the time goes in v1:
time: 101 us
  Pallas kernels  90.6 us (90%)
  local copies, waits for them, and re-layouts  8.97 us (9%)
  between operations  1.31 us (1%)
    pallas_call x1, Pallas kernels, step(): pl.pallas_call(step_kernel, name='step', out_shape=outs, in_specs=[HBM, H...  65.4 us
    pallas_call x1, Pallas kernels, finish(): pl.pallas_call(finish_kernel, name='finish', grid=(rows // tile,), out_sh...  25.2 us
    unnamed x18, local copies, waits for them, and re-layouts  8.97 us

profile of v1, /device:TPU:3, one launch (start us, length us, event | category | flops | bytes accessed | tf_op | source)
XLA Modules:
  0.0 100.9 jit_solution(7843305829055123)
XLA Ops:
  1.3 0.0 copy-start
  1.3 1.5 %copy-done = bf16[256,3584]{1,0:T(8,128)(2,1)S(1)} copy-done((bf16[256,3584]{1,0:T(8,128)(2,1)S(1)}, bf16[256,3584]{1,0:T(8,128)(2,1)}, u32[]{:S(2)}) %copy-start) | copy-done | bytes 1835032
  2.8 0.0 copy-start.1
  2.8 1.2 %copy-done.1 = bf16[256,2048]{1,0:T(8,128)(2,1)S(1)} copy-done((bf16[256,2048]{1,0:T(8,128)(2,1)S(1)}, bf16[256,2048]{1,0:T(8,128)(2,1)}, u32[]{:S(2)}) %copy-start.1) | copy-done | bytes 1048600
  4.0 0.0 copy-start.2
  4.0 1.0 %copy-done.2 = bf16[32,8192]{1,0:T(8,128)(2,1)S(1)} copy-done((bf16[32,8192]{1,0:T(8,128)(2,1)S(1)}, bf16[32,8192]{1,0:T(8,128)(2,1)}, u32[]{:S(2)}) %copy-start.2) | copy-done | bytes 524312
  5.0 0.0 copy-start.3
  5.1 0.9 copy-done.3
  5.9 0.0 copy-start.4
  6.0 0.9 copy-done.4
  6.8 0.0 copy-start.5
  6.8 0.9 copy-done.5
  7.7 0.0 copy-start.6
  7.7 0.8 copy-done.6
  8.6 0.0 copy-start.7
  8.6 0.8 copy-done.7
  9.4 0.0 copy-start.8
  9.4 0.8 copy-done.8
  10.3 65.4 %step.1 = (f32[8,2048]{1,0:T(8,128)S(1)}, f32[8,2048]{1,0:T(8,128)S(1)}, f32[8,2048]{1,0:T(8,128)S(1)}, f32[8,3584]{1,0:T(8,128)S(1)}, f32[8,3584]{1,0:T(8,128)S...) custom-call(bf16[256,2048]{1,0:T(8,128)(2,1)S(1)} %copy-done.1, ...), custom_call_target="tpu_custom_call" | custom-call | flops 1000000000 | bytes 10000000 | tf_op jit(solution)/shard_map/step/pallas_call | solution.py:734
  75.7 25.2 %finish.1 = (bf16[1792,8192]{1,0:T(8,128)(2,1)}, bf16[1792,256]{1,0:T(8,128)(2,1)}, f32[8,2048]{1,0:T(8,128)}, f32[8,2048]{1,0:T(8,128)}, f32[8,2048]{1,0:T(8,12...) custom-call(bf16[1792,8192]{1,0:T(8,128)(2,1)} %base_ref.1, bf16[64,1792]{1,0:T(8,128)(2,1)S(1)} %bitcast.5, ...), custom_call_target="tpu_custom_call" | custom-call | flops 9395240960 | bytes 58720256 | tf_op jit(solution)/shard_map/finish/pallas_call | solution.py:782
Async XLA Ops:
  1.3 1.5 %copy-start = (bf16[256,3584]{1,0:T(8,128)(2,1)S(1)}, bf16[256,3584]{1,0:T(8,128)(2,1)}, u32[]{:S(2)}) copy-start(bf16[256,3584]{1,0:T(8,128)(2,1)} %cot_hbm.1) | copy-start | bytes 5505028
  2.8 1.2 %copy-start.1 = (bf16[256,2048]{1,0:T(8,128)(2,1)S(1)}, bf16[256,2048]{1,0:T(8,128)(2,1)}, u32[]{:S(2)}) copy-start(bf16[256,2048]{1,0:T(8,128)(2,1)} %act_hbm.1) | copy-start | bytes 3145732
  4.0 1.0 %copy-start.2 = (bf16[32,8192]{1,0:T(8,128)(2,1)S(1)}, bf16[32,8192]{1,0:T(8,128)(2,1)}, u32[]{:S(2)}) copy-start(bf16[32,8192]{1,0:T(8,128)(2,1)} %prompts_hbm.1) | copy-start | bytes 1572868
  5.0 0.9 copy-start.3
  5.9 0.9 copy-start.4
  6.8 0.9 copy-start.5
  7.7 0.8 copy-start.6
  8.6 0.8 copy-start.7
  9.4 0.8 copy-start.8

commit v2 on v1

--- a/solution.py
+++ b/solution.py
@@ -437,7 +437,8 @@
 
 HBM = pl.BlockSpec(memory_space=pltpu.HBM)
 SMEM = pl.BlockSpec(memory_space=pltpu.SMEM)
-PARTS = 4
+PARTS = 8
+ACROSS = 0
 
 
 class Wires:
@@ -463,8 +464,8 @@
 
 
 def step_kernel(
-    act_hbm, cot_hbm, keep_ref, a_hbm, am_hbm, av_hbm, b_hbm, bm_hbm, bv_hbm, prompts_hbm,
-    a_new, a_mom, a_sec, b_new, b_mom, b_sec, whole, piece, group,
+    act_hbm, cot_hbm, keep_ref, a_hbm, am_hbm, av_hbm, b_hbm, bm_hbm, bv_hbm, prompts_hbm, base_hbm,
+    a_new, a_mom, a_sec, b_new, b_mom, b_sec, whole, piece, group, base, product,
     act, cot, a, am, av, b, bm, bv, fa, fb, la, lb, ra, rb, pa, pb, xa, xb, sa, sb, za, zb, oa, ob, b_send,
     local, sends, recvs, b_sends, b_recvs,
 ):
@@ -483,6 +484,7 @@
     for i, (name, source, target) in enumerate(pairs):
         loads[name] = pltpu.make_async_copy(source, target, local.at[i])
         loads[name].start()
+    loads["base"] = pltpu.make_async_copy(base_hbm, base, local.at[len(pairs)])
 
     barrier = pltpu.get_barrier_semaphore()
 
@@ -517,8 +519,8 @@
         to_dp = {(j, 0): wires.send(home, home, dp_peer(j)) for j in range(1, dps)}
         return to_role, to_dp
 
-    def gather_forward(ref, to_role, to_dp):
-        for k in near:
+    def gather_forward(ref, to_role, to_dp, steps):
+        for k in steps:
             slot = ref.at[dp, role_back(k)]
             wires.landed(slot, to_role[k])
             for j in range(1, dps):
@@ -531,11 +533,10 @@
     width = prompts_hbm.shape[1] // PARTS
     part = lambda ref, c: ref.at[:, pl.ds(c * width, width)]
     spot = lambda d, t, c: group.at[d, t, :, pl.ds(c * width, width)]
-    via_dp = PARTS // 2
-    hi_own, lo_own, dp_own, hi_far, dp_far, lo_ids = {}, {}, {}, {}, {}, {}
-
-    def prompts_first():
-        for c in range(PARTS):
+    hi_own, lo_own, dp_own, far_ids, lo_ids = {}, {}, {}, {}, {}
+
+    def prompts_near(parts):
+        for c in parts:
             for h in range(1, half):
                 hi_own[h, c] = wires.send(part(prompts_hbm, c), spot(dp, tp, c), tp_peer(2 * h))
             lo_own[c] = wires.send(part(prompts_hbm, c), spot(dp, tp, c), lo_peer)
@@ -551,9 +552,9 @@
                 slot = spot(dp, tp_back(2 * h), c)
                 wires.landed(slot, hi_own[h, c])
                 lo_ids[0, h, c] = wires.send(slot, slot, lo_peer)
-                if c < via_dp:
+                if c >= PARTS - ACROSS:
                     for j in range(1, dps):
-                        dp_far[j, h, c] = wires.send(slot, slot, dp_peer(j))
+                        far_ids[j, h, c] = wires.send(slot, slot, dp_peer(j))
 
     def prompts_dp_landed(parts):
         for c in parts:
@@ -561,37 +562,44 @@
                 slot = spot(dp_back(j), tp, c)
                 wires.landed(slot, dp_own[j, c])
                 lo_ids[j, 0, c] = wires.send(slot, slot, lo_peer)
-                if c >= via_dp:
+                if c < PARTS - ACROSS:
                     for h in range(1, half):
-                        hi_far[j, h, c] = wires.send(slot, slot, tp_peer(2 * h))
-
-    def prompts_far_landed():
-        for c in range(PARTS):
+                        far_ids[j, h, c] = wires.send(slot, slot, tp_peer(2 * h))
+
+    def prompts_far_landed(parts):
+        for c in parts:
             for j in range(1, dps):
                 for h in range(1, half):
                     slot = spot(dp_back(j), tp_back(2 * h), c)
-                    wires.landed(slot, dp_far[j, h, c] if c < via_dp else hi_far[j, h, c])
+                    wires.landed(slot, far_ids[j, h, c])
                     lo_ids[j, h, c] = wires.send(slot, slot, lo_peer)
 
-    def prompts_finish():
-        for c, place in lo_own.items():
-            wires.landed(spot(dp, other, c), place)
-        for (j, h, c), place in lo_ids.items():
-            wires.landed(spot(dp_back(j), lax.rem(other + tps - 2 * h, tps), c), place)
-
-    a_role, a_dp = gather_start(fa)
-    b_role, b_dp = gather_start(fb)
-    prompts_first()
-    gather_forward(fa, a_role, a_dp)
-    gather_forward(fb, b_role, b_dp)
-    prompts_across(range(via_dp))
-
-    def low_start(ref, to_dp, tokens, name, low):
+    def prompts_finish(parts):
+        for c in parts:
+            wires.landed(spot(dp, other, c), lo_own[c])
+            for j in range(dps):
+                for h in range(half):
+                    if (j, h) != (0, 0):
+                        wires.landed(spot(dp_back(j), lax.rem(other + tps - 2 * h, tps), c), lo_ids[j, h, c])
+
+    def multiply(parts):
+        columns = pl.ds(parts[0] * width, len(parts) * width)
+        right = group[:, :, :, columns].reshape(-1, len(parts) * width)
+        tiles = 4
+        tile = product.shape[0] // tiles
+
+        @pl.loop(0, tiles)
+        def _(i):
+            rows = pl.ds(pl.multiple_of(i * tile, tile), tile)
+            term = contract_cols(base[rows, columns], right)
+            product[rows, :] = term if parts[0] == 0 else product[rows, :] + term
+
+    def low_start(ref, to_dp, tokens, name, low, slots):
         gather_finish(ref, to_dp)
         loads[name].wait()
         rows = ref[...].reshape(-1, ref.shape[-1])
         low[...] = contract_cols(rows, tokens[...]).astype(bf16)
-        return [wires.send(low, (ra if low is la else rb).at[k - 1], tp_peer(k)) for k in range(1, tps)]
+        return [wires.send(low, slots.at[k - 1], tp_peer(k)) for k in range(1, tps)]
 
     def low_finish(low, slots, ids):
         total = low[...].astype(f32)
@@ -599,9 +607,6 @@
             wires.landed(slots.at[k - 1], ids[k - 1])
             total = total + slots[k - 1].astype(f32)
         return (total * keep_ref[0].astype(f32)).astype(bf16)
-
-    a_low = low_start(fa, a_dp, act, "act", la)
-    b_low = low_start(fb, b_dp, cot, "cot", lb)
 
     order = far + [0]
 
@@ -614,13 +619,12 @@
                 ids[j, k] = wires.send(ref.at[dp_of(j), role_of(k)], x_slots.at[j - 1, role_of(k)], dp_peer(j))
         return ids
 
-    def reduce_middle(ref, x_slots, x_ids, s_slots, z_slots, own):
+    def reduce_middle(ref, x_slots, x_ids, s_slots, z_slots, own, steps):
         ids = {}
-        for k in order:
+        for k in steps:
             total = ref[dp, role_of(k)].astype(f32)
             for j in range(1, dps):
-                wires.landed(x_slots.at[j - 1, role], x_ids[j, k]) if k == 0 else wires.landed(
-                    x_slots.at[j - 1, role_of(k)], x_ids[j, k])
+                wires.landed(x_slots.at[j - 1, role_of(k)], x_ids[j, k])
                 total = total + x_slots[j - 1, role_of(k)].astype(f32)
             if k == 0:
                 own[...] = total
@@ -631,29 +635,10 @@
 
     def reduce_finish(own, z_slots, ids):
         total = own[...]
-        for k in order[:-1]:
+        for k in near:
             wires.landed(z_slots.at[k - 1], ids[k])
             total = total + z_slots[k - 1].astype(f32)
         return total * scale
-
-    kept_in = low_finish(la, ra, a_low)
-    xb_ids = reduce_start(pb, kept_in, cot, xb)
-    kept_grad = low_finish(lb, rb, b_low)
-    xa_ids = reduce_start(pa, kept_grad, act, xa)
-    prompts_hi_landed(range(PARTS))
-    zb_ids = reduce_middle(pb, xb, xb_ids, sb, zb, ob)
-    za_ids = reduce_middle(pa, xa, xa_ids, sa, za, oa)
-    prompts_across(range(via_dp, PARTS))
-    prompts_dp_landed(range(via_dp))
-
-    for name in ("am", "av", "bm", "bv"):
-        loads[name].wait()
-
-    fresh, mom, sec = adam_update(b[...], bm[...], bv[...], reduce_finish(ob, zb, zb_ids))
-    b_new[...], b_mom[...], b_sec[...] = fresh, mom, sec
-    columns = fresh.shape[1] // dps
-    for i in range(dps):
-        b_send[i] = fresh[:, i * columns : (i + 1) * columns].astype(bf16)
 
     def b_copy(i, k):
         block = tp * dps + i
@@ -668,55 +653,113 @@
         here = (block // tps == dp) & (lax.rem(block, tps) == tp)
         return here, remote, pltpu.make_async_copy(b_send.at[i], place, b_recvs.at[dp, role])
 
-    for k in far + [0]:
-        for i in range(dps):
-            here, remote, beside = b_copy(i, k)
-            if here is None:
-                remote.start()
-            else:
-                pl.when(here)(beside.start)
-                pl.when(jnp.logical_not(here))(remote.start)
-
+    def b_start():
+        for k in order:
+            for i in range(dps):
+                here, remote, beside = b_copy(i, k)
+                if here is None:
+                    remote.start()
+                else:
+                    pl.when(here)(beside.start)
+                    pl.when(jnp.logical_not(here))(remote.start)
+
+    def b_finish():
+        for d in range(dps):
+            for r in range(roles):
+                landed(piece.at[d, r], b_recvs.at[d, r])
+        for k in range(roles):
+            for i in range(dps):
+                here, remote, _ = b_copy(i, k)
+                if here is None:
+                    remote.wait_send()
+                else:
+                    pl.when(jnp.logical_not(here))(remote.wait_send)
+
+    first, second, third, fourth = [range(i * PARTS // 4, (i + 1) * PARTS // 4) for i in range(4)]
+
+    b_role, b_dp = gather_start(fb)
+    a_role, a_dp = gather_start(fa)
+    prompts_near(range(PARTS))
+    prompts_across(first)
+    gather_forward(fb, b_role, b_dp, near)
+    loads["base"].start()
+    gather_forward(fa, a_role, a_dp, near[:-1])
+    b_low = low_start(fb, b_dp, cot, "cot", lb, rb)
+    gather_forward(fa, a_role, a_dp, near[-1:])
+    prompts_across(second)
+    a_low = low_start(fa, a_dp, act, "act", la, ra)
+
+    kept_grad = low_finish(lb, rb, b_low)
+    xa_ids = reduce_start(pa, kept_grad, act, xa)
+    kept_in = low_finish(la, ra, a_low)
+    xb_ids = reduce_start(pb, kept_in, cot, xb)
+    prompts_across(third)
+    prompts_dp_landed(first)
+    za_ids = reduce_middle(pa, xa, xa_ids, sa, za, oa, order)
+    prompts_hi_landed(range(PARTS))
+    zb_ids = reduce_middle(pb, xb, xb_ids, sb, zb, ob, order[:2])
+    prompts_dp_landed(second)
+
+    for name in ("am", "av", "bm", "bv"):
+        loads[name].wait()
     fresh, mom, sec = adam_update(a[...], am[...], av[...], reduce_finish(oa, za, za_ids))
     whole[tp, dp, role] = fresh.astype(bf16)
     a_new[...], a_mom[...], a_sec[...] = fresh, mom, sec
+
     mine = whole.at[tp]
+    hi_ids, lo_a = {}, {}
+
+    def onward(j, k):
+        slot = mine.at[dp_back(j), role_back(k)]
+        for h in range(1, half):
+            hi_ids[h, j, k] = wires.send(slot, slot, tp_peer(2 * h))
+        lo_a[0, j, k] = wires.send(slot, slot, lo_peer)
+
     a_role, a_dp = gather_start(mine)
-    gather_forward(mine, a_role, a_dp)
-    hi_ids, lo_a = {}, {}
+    onward(0, 0)
+    zb_ids.update(reduce_middle(pb, xb, xb_ids, sb, zb, ob, order[2:]))
+    for k in near:
+        gather_forward(mine, a_role, a_dp, [k])
+        onward(0, k)
+    prompts_across(fourth)
+
+    fresh, mom, sec = adam_update(b[...], bm[...], bv[...], reduce_finish(ob, zb, zb_ids))
+    b_new[...], b_mom[...], b_sec[...] = fresh, mom, sec
+    columns = fresh.shape[1] // dps
+    for i in range(dps):
+        b_send[i] = fresh[:, i * columns : (i + 1) * columns].astype(bf16)
+    b_start()
+    for j in range(1, dps):
+        for k in [0] + near:
+            wires.landed(mine.at[dp_back(j), role_back(k)], a_dp[j, k])
+            onward(j, k)
+    prompts_dp_landed(third)
+    loads["own"].wait()
+    loads["base"].wait()
+    prompts_far_landed(first)
+    prompts_far_landed(second)
+    prompts_finish(first)
+    prompts_finish(second)
+    multiply([*first, *second])
+    prompts_dp_landed(fourth)
     for j in range(dps):
-        if j > 0:
-            for k in range(roles):
-                wires.landed(mine.at[dp_back(j), role_back(k)], a_dp[j, k])
-        slot = mine.at[dp_back(j)]
-        for h in range(1, half):
-            hi_ids[h, j] = wires.send(slot, slot, tp_peer(2 * h))
-        lo_a[0, j] = wires.send(slot, slot, lo_peer)
-    prompts_dp_landed(range(via_dp, PARTS))
-    prompts_far_landed()
-    for j in range(dps):
-        for h in range(1, half):
-            slot = whole.at[tp_back(2 * h), dp_back(j)]
-            wires.landed(slot, hi_ids[h, j])
-            lo_a[h, j] = wires.send(slot, slot, lo_peer)
-    for (h, j), place in lo_a.items():
-        wires.landed(whole.at[lax.rem(other + tps - 2 * h, tps), dp_back(j)], place)
-    for d in range(dps):
-        for r in range(roles):
-            landed(piece.at[d, r], b_recvs.at[d, r])
-    prompts_finish()
-    loads["own"].wait()
-    for k in range(roles):
-        for i in range(dps):
-            here, remote, _ = b_copy(i, k)
-            if here is None:
-                remote.wait_send()
-            else:
-                pl.when(jnp.logical_not(here))(remote.wait_send)
+        for k in [0] + near:
+            for h in range(1, half):
+                slot = whole.at[tp_back(2 * h), dp_back(j), role_back(k)]
+                wires.landed(slot, hi_ids[h, j, k])
+                lo_a[h, j, k] = wires.send(slot, slot, lo_peer)
+    prompts_far_landed(third)
+    prompts_far_landed(fourth)
+    prompts_finish(third)
+    prompts_finish(fourth)
+    multiply([*third, *fourth])
+    for (h, j, k), place in lo_a.items():
+        wires.landed(whole.at[lax.rem(other + tps - 2 * h, tps), dp_back(j), role_back(k)], place)
+    b_finish()
     wires.drain()
 
 
-def step(activations, cotangent, block_keep, a, am, av, b, bm, bv, prompts):
+def step(activations, cotangent, block_keep, a, am, av, b, bm, bv, prompts, base):
     roles, dps, tps = sizes()
     tokens, a_width = activations.shape
     b_width = cotangent.shape[1]
@@ -724,18 +767,21 @@
     rank = roles * dps * rows
     bf16, f32 = jnp.bfloat16, jnp.float32
     vmem = pltpu.VMEM
-    args = [activations, cotangent, block_keep, a, am, av, b, bm, bv, prompts]
-    outs = [jax.ShapeDtypeStruct(x.shape, f32) for x in (a, a, a, b, b, b)] + [
-        jax.ShapeDtypeStruct((tps, dps, roles, rows, a_width), bf16),
-        jax.ShapeDtypeStruct((dps, roles, rows, b_width // dps), bf16),
-        jax.ShapeDtypeStruct((dps, tps, *prompts.shape), bf16),
+    args = [activations, cotangent, block_keep, a, am, av, b, bm, bv, prompts, base]
+    args = [x if x is block_keep else pltpu.with_memory_space_constraint(x, pltpu.HBM) for x in args]
+    outs = [vmem(x.shape, f32) for x in (a, a, a, b, b, b)] + [
+        vmem((tps, dps, roles, rows, a_width), bf16),
+        vmem((dps, roles, rows, b_width // dps), bf16),
+        vmem((dps, tps, *prompts.shape), bf16),
+        vmem(base.shape, bf16),
+        vmem((base.shape[0], dps * tps * prompts.shape[0]), f32),
     ]
     wide = lambda *lead: [vmem((*lead, rows, w), bf16) for w in (a_width, b_width)]
     return pl.pallas_call(
         step_kernel,
         name="step",
         out_shape=outs,
-        in_specs=[HBM, HBM, SMEM] + [HBM] * 7,
+        in_specs=[HBM, HBM, SMEM] + [HBM] * 8,
         out_specs=[VMEM] * len(outs),
         scratch_shapes=[vmem(activations.shape, bf16), vmem(cotangent.shape, bf16)]
         + [vmem(a.shape, f32)] * 3
@@ -748,61 +794,88 @@
         + wide(roles - 1)
         + wide(roles - 1)
         + [vmem(a.shape, f32), vmem(b.shape, f32), vmem((dps, rows, b_width // dps), bf16)]
-        + [dma(9), dma(160), dma(160), dma(dps, roles), dma(dps, roles)],
+        + [dma(10), dma(240), dma(240), dma(dps, roles), dma(dps, roles)],
         compiler_params=pltpu.CompilerParams(
-            collective_id=0, has_side_effects=True, vmem_limit_bytes=40 * 1024 * 1024
+            collective_id=0, has_side_effects=True, vmem_limit_bytes=16 * 1024 * 1024
         ),
         cost_estimate=pl.CostEstimate(flops=10**9, bytes_accessed=10**7, transcendentals=0),
     )(*args)
 
 
-def finish_kernel(base_ref, b_ref, a_ref, prompts_ref, *refs):
-    small, (merged_ref, projected_ref), copies = refs[:6], refs[6:8], refs[8:]
-
-    @pl.when(pl.program_id(0) == 0)
-    def _():
-        for source, target in zip(small, copies):
-            target[...] = source[...]
-
-    shards, _, width = a_ref.shape
-    total = jnp.zeros(projected_ref.shape, jnp.float32)
+def finish_kernel(*refs):
+    small, (base, b, a, prompts, product) = refs[:6], refs[6:11]
+    copies, (merged_hbm, projected_hbm) = refs[11:17], refs[17:19]
+    stage, projected, sems, out_sems, small_sems = refs[19:]
+    saves = [pltpu.make_async_copy(x, y, small_sems.at[i]) for i, (x, y) in enumerate(zip(small, copies))]
+    for save in saves:
+        save.start()
+    depth, shards, tile, width = stage.shape
+    tiles = base.shape[0] // tile
+
+    def out(i, shard):
+        rows = pl.ds(pl.multiple_of(i * tile, tile), tile)
+        slot = lax.rem(i, depth)
+        target = merged_hbm.at[rows, shard * width : (shard + 1) * width]
+        return pltpu.make_async_copy(stage.at[slot, shard], target, sems.at[slot, shard])
+
+    @pl.loop(0, tiles)
+    def _(i):
+        rows = pl.ds(pl.multiple_of(i * tile, tile), tile)
+        left = b[:, rows] * adapter_scale
+        for shard in range(shards):
+
+            @pl.when(i >= depth)
+            def _():
+                out(i - depth, shard).wait()
+
+        for shard in range(shards):
+            delta = contract_rows(left, a[shard])
+            merged = base[rows, shard * width : (shard + 1) * width].astype(jnp.float32) + delta
+            stage[lax.rem(i, depth), shard] = merged.astype(stage.dtype)
+            out(i, shard).start()
+
+    low = jnp.zeros((a.shape[1], prompts.shape[0]), jnp.float32)
     for shard in range(shards):
-        columns = pl.ds(shard * width, width)
-        delta = contract_rows(b_ref[...], a_ref[shard])
-        merged = (base_ref[:, columns].astype(jnp.float32) + adapter_scale * delta).astype(jnp.bfloat16)
-        merged_ref[:, columns] = merged
-        total = total + contract_cols(merged, prompts_ref[:, columns])
-    projected_ref[...] = total.astype(projected_ref.dtype)
-
-
-def finish(base, b, a, prompts, small):
+        low = low + contract_cols(a[shard], prompts[:, shard * width : (shard + 1) * width])
+    high = low.astype(jnp.bfloat16)
+    rest = (low - high.astype(jnp.float32)).astype(jnp.bfloat16)
+
+    saved = []
+    for i in range(base.shape[0] // tile):
+        rows = pl.ds(i * tile, tile)
+        extra = contract_rows(b[:, rows], high) + contract_rows(b[:, rows], rest)
+        projected[rows, :] = (product[rows, :] + adapter_scale * extra).astype(projected.dtype)
+    last = pltpu.make_async_copy(projected, projected_hbm, out_sems.at[0])
+    last.start()
+
+    for i in range(max(tiles - depth, 0), tiles):
+        for shard in range(shards):
+            out(i, shard).wait()
+
+    for save in saves + [last]:
+        save.wait()
+
+
+def finish(base, b, a, prompts, product, small):
     rows, width = base.shape
     tile = max(t for t in range(128, 257, 128) if rows % t == 0)
     count = prompts.shape[0]
+    shards, _, part = a.shape
+    vmem = pltpu.VMEM
+    args = [pltpu.with_memory_space_constraint(x, pltpu.VMEM) for x in (*small, base, b, a, prompts, product)]
     return pl.pallas_call(
         finish_kernel,
         name="finish",
-        grid=(rows // tile,),
-        out_shape=[
-            jax.ShapeDtypeStruct(base.shape, base.dtype),
-            jax.ShapeDtypeStruct((rows, count), jnp.bfloat16),
-        ]
-        + [jax.ShapeDtypeStruct(x.shape, x.dtype) for x in small],
-        in_specs=[
-            pl.BlockSpec((tile, width), lambda i: (i, 0)),
-            pl.BlockSpec((b.shape[0], tile), lambda i: (0, i)),
-        ]
-        + [VMEM] * (2 + len(small)),
-        out_specs=[
-            pl.BlockSpec((tile, width), lambda i: (i, 0)),
-            pl.BlockSpec((tile, count), lambda i: (i, 0)),
-        ]
-        + [VMEM] * len(small),
-        compiler_params=pltpu.CompilerParams(vmem_limit_bytes=40 * 1024 * 1024),
+        out_shape=[pltpu.HBM(x.shape, x.dtype) for x in (*small, base)]
+        + [pltpu.HBM((rows, count), jnp.bfloat16)],
+        in_specs=[VMEM] * len(args),
+        out_specs=[HBM] * (len(small) + 2),
+        scratch_shapes=[vmem((2, shards, tile, part), base.dtype), vmem((rows, count), jnp.bfloat16), dma(2, shards), dma(1), dma(len(small))],
+        compiler_params=pltpu.CompilerParams(vmem_limit_bytes=16 * 1024 * 1024),
         cost_estimate=pl.CostEstimate(
             flops=2 * rows * width * (count + b.shape[0]), bytes_accessed=4 * rows * width, transcendentals=0
         ),
-    )(base, b, a, prompts, *small)
+    )(*args)
 
 
 def fused_body(
@@ -811,15 +884,16 @@
 ):
     roles, dps, tps = sizes()
     rank = roles * dps * input_factor.shape[0]
-    *small, whole, piece, group = step(
+    *small, whole, piece, group, base, product = step(
         activations, cotangent, block_keep, input_factor, input_mean, input_square,
-        output_factor, output_mean, output_square, prompts,
-    )
-    merged, projected, *copies = finish(
-        frozen_base_rows,
+        output_factor, output_mean, output_square, prompts, frozen_base_rows,
+    )
+    *copies, merged, projected = finish(
+        base,
         piece.reshape(rank, -1),
         whole.reshape(tps, rank, -1),
         group.reshape(-1, prompts.shape[1]),
+        product,
         small,
     )
     a_new, a_mom, a_sec, b_new, b_mom, b_sec = copies

time: 101 us -> 78.5 us (0.78)
  Pallas kernels: 90.6 us -> 76.8 us
  local copies, waits for them, and re-layouts: 8.97 us -> 0 us
    pallas_call x1, Pallas kernels: 25.2 us -> 12.8 us  [finish(): pl.pallas_call(finish_kernel, name='finish', out_shape=[pltpu.HBM(x.shape...]
    unnamed x18 -> x0, local copies, waits for them, and re-layouts: 8.97 us -> none
    pallas_call x1, Pallas kernels: 65.4 us -> 64 us  [step(): pl.pallas_call(step_kernel, name='step', out_shape=outs, in_specs=[HBM, H...]
where the time goes in v2:
time: 78.5 us; the launch traced here: 78.1 us
  Pallas kernels  76.8 us (98%)
  between operations  1.29 us (2%)
    pallas_call x1, Pallas kernels, step(): pl.pallas_call(step_kernel, name='step', out_shape=outs, in_specs=[HBM, H...  64 us
    pallas_call x1, Pallas kernels, finish(): pl.pallas_call(finish_kernel, name='finish', out_shape=[pltpu.HBM(x.shape...  12.8 us

profile of v2, /device:TPU:3, one launch (start us, length us, event | category | flops | bytes accessed | tf_op | source)
XLA Modules:
  0.0 78.1 jit_solution(11693410161780070697)
XLA Ops:
  1.3 64.0 %step.1 = (f32[8,2048]{1,0:T(8,128)S(1)}, f32[8,2048]{1,0:T(8,128)S(1)}, f32[8,2048]{1,0:T(8,128)S(1)}, f32[8,3584]{1,0:T(8,128)S(1)}, f32[8,3584]{1,0:T(8,128)S...) custom-call(bf16[256,2048]{1,0:T(8,128)(2,1)} %act_hbm.1, ...), custom_call_target="tpu_custom_call" | custom-call | flops 1000000000 | bytes 10000000 | tf_op jit(solution)/shard_map/step/pallas_call | solution.py:780
  65.3 12.8 %finish.1 = (f32[8,2048]{1,0:T(8,128)}, f32[8,2048]{1,0:T(8,128)}, f32[8,2048]{1,0:T(8,128)}, f32[8,3584]{1,0:T(8,128)}, f32[8,3584]{1,0:T(8,128)}, /*index=5*/f...) custom-call(f32[8,2048]{1,0:T(8,128)S(1)} %get-tuple-element.27.refs_0_, ...), custom_call_target="tpu_custom_call" | custom-call | flops 9395240960 | bytes 58720256 | tf_op jit(solution)/shard_map/finish/pallas_call | solution.py:866

commit v3 on v2

--- a/solution.py
+++ b/solution.py
@@ -1,4 +1,5 @@
 import functools
+import math
 
 import jax
 import jax.numpy as jnp
@@ -437,26 +438,33 @@
 
 HBM = pl.BlockSpec(memory_space=pltpu.HBM)
 SMEM = pl.BlockSpec(memory_space=pltpu.SMEM)
-PARTS = 8
-ACROSS = 0
+PARTS = 4
+ARRIVALS = 66
 
 
 class Wires:
-    def __init__(self, sends, recvs):
-        self.sends, self.recvs, self.copies, self.used = sends, recvs, [], 0
-
-    def send(self, source, target, peer):
-        place = self.used
+    def __init__(self, sends, recvs, ruler):
+        self.sends, self.recvs, self.ruler, self.used, self.sent = sends, recvs, ruler, 0, 0
+
+    def take(self):
         self.used += 1
-        self.copies.append(send(source, target, self.sends.at[place], self.recvs.at[place], peer))
+        return self.used - 1
+
+    def send(self, source, target, peer, place=None):
+        place = self.take() if place is None else place
+        send(source, target, self.sends.at[0], self.recvs.at[place], peer)
+        self.sent += math.prod(source.shape) * source.dtype.itemsize
         return place
 
     def landed(self, slot, place):
         landed(slot, self.recvs.at[place])
 
     def drain(self):
-        for copy in self.copies:
-            copy.wait_send()
+        rows, width = self.ruler.shape
+        tiles, rest = divmod(self.sent, 8 * 128 * self.ruler.dtype.itemsize)
+        wide = max(w for w in range(1, width // 128 + 1) if tiles % w == 0)
+        assert rest == 0 and tiles // wide * 8 <= rows
+        landed(self.ruler.at[pl.ds(0, tiles // wide * 8), pl.ds(0, wide * 128)], self.sends.at[0])
 
 
 def far_first(count):
@@ -476,7 +484,7 @@
     me = (role * dps + dp) * tps + tp
     scale = adapter_scale / ROLLOUT_TOKENS
     bf16, f32 = jnp.bfloat16, jnp.float32
-    wires = Wires(sends, recvs)
+    wires = Wires(sends, recvs, base_hbm)
 
     loads = {}
     pairs = [("a", a_hbm, a), ("b", b_hbm, b), ("act", act_hbm, act), ("cot", cot_hbm, cot), ("am", am_hbm, am),
@@ -533,13 +541,14 @@
     width = prompts_hbm.shape[1] // PARTS
     part = lambda ref, c: ref.at[:, pl.ds(c * width, width)]
     spot = lambda d, t, c: group.at[d, t, :, pl.ds(c * width, width)]
-    hi_own, lo_own, dp_own, far_ids, lo_ids = {}, {}, {}, {}, {}
+    hi_own, dp_own, far_ids = {}, {}, {}
+    shared = [wires.take() for _ in range(PARTS)]
 
     def prompts_near(parts):
         for c in parts:
             for h in range(1, half):
                 hi_own[h, c] = wires.send(part(prompts_hbm, c), spot(dp, tp, c), tp_peer(2 * h))
-            lo_own[c] = wires.send(part(prompts_hbm, c), spot(dp, tp, c), lo_peer)
+            wires.send(part(prompts_hbm, c), spot(dp, tp, c), lo_peer, shared[c])
 
     def prompts_across(parts):
         for c in parts:
@@ -551,20 +560,16 @@
             for h in range(1, half):
                 slot = spot(dp, tp_back(2 * h), c)
                 wires.landed(slot, hi_own[h, c])
-                lo_ids[0, h, c] = wires.send(slot, slot, lo_peer)
-                if c >= PARTS - ACROSS:
-                    for j in range(1, dps):
-                        far_ids[j, h, c] = wires.send(slot, slot, dp_peer(j))
+                wires.send(slot, slot, lo_peer, shared[c])
 
     def prompts_dp_landed(parts):
         for c in parts:
             for j in range(1, dps):
                 slot = spot(dp_back(j), tp, c)
                 wires.landed(slot, dp_own[j, c])
-                lo_ids[j, 0, c] = wires.send(slot, slot, lo_peer)
-                if c < PARTS - ACROSS:
-                    for h in range(1, half):
-                        far_ids[j, h, c] = wires.send(slot, slot, tp_peer(2 * h))
+                wires.send(slot, slot, lo_peer, shared[c])
+                for h in range(1, half):
+                    far_ids[j, h, c] = wires.send(slot, slot, tp_peer(2 * h))
 
     def prompts_far_landed(parts):
         for c in parts:
@@ -572,30 +577,25 @@
                 for h in range(1, half):
                     slot = spot(dp_back(j), tp_back(2 * h), c)
                     wires.landed(slot, far_ids[j, h, c])
-                    lo_ids[j, h, c] = wires.send(slot, slot, lo_peer)
-
-    def prompts_finish(parts):
-        for c in parts:
-            wires.landed(spot(dp, other, c), lo_own[c])
-            for j in range(dps):
-                for h in range(half):
-                    if (j, h) != (0, 0):
-                        wires.landed(spot(dp_back(j), lax.rem(other + tps - 2 * h, tps), c), lo_ids[j, h, c])
-
-    def multiply(parts):
-        columns = pl.ds(parts[0] * width, len(parts) * width)
-        right = group[:, :, :, columns].reshape(-1, len(parts) * width)
-        tiles = 4
-        tile = product.shape[0] // tiles
-
-        @pl.loop(0, tiles)
+                    wires.send(slot, slot, lo_peer, shared[c])
+
+    def prompts_finish(c):
+        wires.landed(group.at[:, pl.ds(0, half), :, pl.ds(c * width, width)], shared[c])
+
+    tiles = 4
+    tile = product.shape[0] // tiles
+
+    def multiply(c, start, stop):
+        columns = pl.ds(c * width, width)
+        right = group[:, :, :, columns].reshape(-1, width)
+
+        @pl.loop(start, stop)
         def _(i):
             rows = pl.ds(pl.multiple_of(i * tile, tile), tile)
             term = contract_cols(base[rows, columns], right)
-            product[rows, :] = term if parts[0] == 0 else product[rows, :] + term
-
-    def low_start(ref, to_dp, tokens, name, low, slots):
-        gather_finish(ref, to_dp)
+            product[rows, :] = term if c == 0 else product[rows, :] + term
+
+    def low_start(ref, tokens, name, low, slots):
         loads[name].wait()
         rows = ref[...].reshape(-1, ref.shape[-1])
         low[...] = contract_cols(rows, tokens[...]).astype(bf16)
@@ -675,30 +675,45 @@
                 else:
                     pl.when(jnp.logical_not(here))(remote.wait_send)
 
-    first, second, third, fourth = [range(i * PARTS // 4, (i + 1) * PARTS // 4) for i in range(4)]
-
     b_role, b_dp = gather_start(fb)
-    a_role, a_dp = gather_start(fa)
+    a_home = fa.at[dp, role]
+    a_dp = {j: wires.send(a_home, a_home, dp_peer(j)) for j in range(1, dps)}
+    a_role = {(0, k): wires.send(a_home, a_home, role_peer(k)) for k in near}
     prompts_near(range(PARTS))
-    prompts_across(first)
-    gather_forward(fb, b_role, b_dp, near)
+    prompts_across([0])
+    gather_forward(fb, b_role, b_dp, near[:1])
+    for j in range(1, dps):
+        slot = fa.at[dp_back(j), role]
+        wires.landed(slot, a_dp[j])
+        for k in near:
+            a_role[j, k] = wires.send(slot, slot, role_peer(k))
+    gather_forward(fb, b_role, b_dp, near[1:])
     loads["base"].start()
-    gather_forward(fa, a_role, a_dp, near[:-1])
-    b_low = low_start(fb, b_dp, cot, "cot", lb, rb)
-    gather_forward(fa, a_role, a_dp, near[-1:])
-    prompts_across(second)
-    a_low = low_start(fa, a_dp, act, "act", la, ra)
+    prompts_across([1])
+    gather_finish(fb, b_dp)
+    b_low = low_start(fb, cot, "cot", lb, rb)
+    prompts_across([2])
+    for (j, k), place in a_role.items():
+        wires.landed(fa.at[dp_back(j), role_back(k)], place)
+    a_low = low_start(fa, act, "act", la, ra)
+    prompts_across([3])
+    prompts_dp_landed([0, 1])
 
     kept_grad = low_finish(lb, rb, b_low)
     xa_ids = reduce_start(pa, kept_grad, act, xa)
     kept_in = low_finish(la, ra, a_low)
     xb_ids = reduce_start(pb, kept_in, cot, xb)
-    prompts_across(third)
-    prompts_dp_landed(first)
+    prompts_dp_landed([2])
+    prompts_hi_landed(range(PARTS))
+    prompts_far_landed([0])
     za_ids = reduce_middle(pa, xa, xa_ids, sa, za, oa, order)
-    prompts_hi_landed(range(PARTS))
+    prompts_dp_landed([3])
+    loads["own"].wait()
+    loads["base"].wait()
+    prompts_finish(0)
+    multiply(0, 0, 4)
     zb_ids = reduce_middle(pb, xb, xb_ids, sb, zb, ob, order[:2])
-    prompts_dp_landed(second)
+    prompts_far_landed([1])
 
     for name in ("am", "av", "bm", "bv"):
         loads[name].wait()
@@ -707,21 +722,36 @@
     a_new[...], a_mom[...], a_sec[...] = fresh, mom, sec
 
     mine = whole.at[tp]
-    hi_ids, lo_a = {}, {}
+    hi_ids, lo_a = {}, wires.take()
 
     def onward(j, k):
         slot = mine.at[dp_back(j), role_back(k)]
         for h in range(1, half):
             hi_ids[h, j, k] = wires.send(slot, slot, tp_peer(2 * h))
-        lo_a[0, j, k] = wires.send(slot, slot, lo_peer)
+        wires.send(slot, slot, lo_peer, lo_a)
+
+    def beside(j, k):
+        for h in range(1, half):
+            slot = whole.at[tp_back(2 * h), dp_back(j), role_back(k)]
+            wires.landed(slot, hi_ids[h, j, k])
+            wires.send(slot, slot, lo_peer, lo_a)
 
     a_role, a_dp = gather_start(mine)
     onward(0, 0)
     zb_ids.update(reduce_middle(pb, xb, xb_ids, sb, zb, ob, order[2:]))
-    for k in near:
-        gather_forward(mine, a_role, a_dp, [k])
+    prompts_far_landed([2])
+    prompts_finish(1)
+    multiply(1, 0, 3)
+    gather_forward(mine, a_role, a_dp, near[:1])
+    onward(0, near[0])
+    multiply(1, 3, 4)
+    gather_forward(mine, a_role, a_dp, near[1:2])
+    for k in near[1:2]:
         onward(0, k)
-    prompts_across(fourth)
+    prompts_far_landed([3])
+    gather_forward(mine, a_role, a_dp, near[2:])
+    for k in near[2:]:
+        onward(0, k)
 
     fresh, mom, sec = adam_update(b[...], bm[...], bv[...], reduce_finish(ob, zb, zb_ids))
     b_new[...], b_mom[...], b_sec[...] = fresh, mom, sec
@@ -729,34 +759,23 @@
     for i in range(dps):
         b_send[i] = fresh[:, i * columns : (i + 1) * columns].astype(bf16)
     b_start()
+    prompts_finish(2)
     for j in range(1, dps):
         for k in [0] + near:
             wires.landed(mine.at[dp_back(j), role_back(k)], a_dp[j, k])
             onward(j, k)
-    prompts_dp_landed(third)
-    loads["own"].wait()
-    loads["base"].wait()
-    prompts_far_landed(first)
-    prompts_far_landed(second)
-    prompts_finish(first)
-    prompts_finish(second)
-    multiply([*first, *second])
-    prompts_dp_landed(fourth)
-    for j in range(dps):
+    multiply(2, 0, 4)
+    prompts_finish(3)
+    for k in [0] + near:
+        beside(0, k)
+    multiply(3, 0, 4)
+    for j in range(1, dps):
         for k in [0] + near:
-            for h in range(1, half):
-                slot = whole.at[tp_back(2 * h), dp_back(j), role_back(k)]
-                wires.landed(slot, hi_ids[h, j, k])
-                lo_a[h, j, k] = wires.send(slot, slot, lo_peer)
-    prompts_far_landed(third)
-    prompts_far_landed(fourth)
-    prompts_finish(third)
-    prompts_finish(fourth)
-    multiply([*third, *fourth])
-    for (h, j, k), place in lo_a.items():
-        wires.landed(whole.at[lax.rem(other + tps - 2 * h, tps), dp_back(j), role_back(k)], place)
+            beside(j, k)
+    wires.landed(whole.at[pl.ds(0, half)], lo_a)
     b_finish()
     wires.drain()
+    assert wires.used == recvs.shape[0], wires.used
 
 
 def step(activations, cotangent, block_keep, a, am, av, b, bm, bv, prompts, base):
@@ -794,7 +813,7 @@
         + wide(roles - 1)
         + wide(roles - 1)
         + [vmem(a.shape, f32), vmem(b.shape, f32), vmem((dps, rows, b_width // dps), bf16)]
-        + [dma(10), dma(240), dma(240), dma(dps, roles), dma(dps, roles)],
+        + [dma(10), dma(1), dma(ARRIVALS), dma(dps, roles), dma(dps, roles)],
         compiler_params=pltpu.CompilerParams(
             collective_id=0, has_side_effects=True, vmem_limit_bytes=16 * 1024 * 1024
         ),

time: 78.5 us -> 69 us (0.88)
  the two profiles are of different devices: /device:TPU:3 before, /device:TPU:0 now
where the time goes in v3:
time: 69 us; the launch traced here: 68.8 us
  Pallas kernels  67.5 us (98%)
  between operations  1.29 us (2%)
    pallas_call x1, Pallas kernels, step(): pl.pallas_call(step_kernel, name='step', out_shape=outs, in_specs=[HBM, H...  54.7 us
    pallas_call x1, Pallas kernels, finish(): pl.pallas_call(finish_kernel, name='finish', out_shape=[pltpu.HBM(x.shape...  12.8 us

profile of v3, /device:TPU:0, one launch (start us, length us, event | category | flops | bytes accessed | tf_op | source)
XLA Modules:
  0.0 68.8 jit_solution(5152359821611949846)
XLA Ops:
  1.3 54.7 %step.1 = (f32[8,2048]{1,0:T(8,128)S(1)}, f32[8,2048]{1,0:T(8,128)S(1)}, f32[8,2048]{1,0:T(8,128)S(1)}, f32[8,3584]{1,0:T(8,128)S(1)}, f32[8,3584]{1,0:T(8,128)S...) custom-call(bf16[256,2048]{1,0:T(8,128)(2,1)} %act_hbm.1, ...), custom_call_target="tpu_custom_call" | custom-call | flops 1000000000 | bytes 10000000 | tf_op jit(solution)/shard_map/step/pallas_call | solution.py:799
  56.0 12.8 %finish.1 = (f32[8,2048]{1,0:T(8,128)}, f32[8,2048]{1,0:T(8,128)}, f32[8,2048]{1,0:T(8,128)}, f32[8,3584]{1,0:T(8,128)}, f32[8,3584]{1,0:T(8,128)}, /*index=5*/f...) custom-call(f32[8,2048]{1,0:T(8,128)S(1)} %get-tuple-element.27.refs_0_, ...), custom_call_target="tpu_custom_call" | custom-call | flops 9395240960 | bytes 58720256 | tf_op jit(solution)/shard_map/finish/pallas_call | solution.py:885

commit v4 on v3

--- a/solution.py
+++ b/solution.py
@@ -480,8 +480,6 @@
     role, dp, tp = places()
     roles, dps, tps = sizes()
     half = tps // 2
-    devices = roles * dps * tps
-    me = (role * dps + dp) * tps + tp
     scale = adapter_scale / ROLLOUT_TOKENS
     bf16, f32 = jnp.bfloat16, jnp.float32
     wires = Wires(sends, recvs, base_hbm)
@@ -493,20 +491,20 @@
         loads[name] = pltpu.make_async_copy(source, target, local.at[i])
         loads[name].start()
     loads["base"] = pltpu.make_async_copy(base_hbm, base, local.at[len(pairs)])
+    loads["base"].start()
 
     barrier = pltpu.get_barrier_semaphore()
-
-    @pl.loop(1, devices)
-    def _(step):
-        other = lax.rem(me + step, devices)
-        peer = (other // (dps * tps), lax.rem(other // tps, dps), lax.rem(other, tps))
+    around = [(lax.rem(role + k, roles), dp, tp) for k in range(1, roles)]
+    around += [(role, lax.rem(dp + j, dps), tp) for j in range(1, dps)]
+    around += [(role, dp, lax.rem(tp + k, tps)) for k in range(1, tps)]
+    for peer in around:
         pl.semaphore_signal(barrier, inc=1, device_id=peer, device_id_type=MESH)
 
     loads["a"].wait()
     fa[dp, role] = a[...].astype(bf16)
     loads["b"].wait()
     fb[dp, role] = b[...].astype(bf16)
-    pl.semaphore_wait(barrier, devices - 1)
+    pl.semaphore_wait(barrier, len(around))
 
     role_of = lambda k: lax.rem(role + k, roles)
     role_back = lambda k: lax.rem(role + roles - k, roles)
@@ -582,7 +580,7 @@
     def prompts_finish(c):
         wires.landed(group.at[:, pl.ds(0, half), :, pl.ds(c * width, width)], shared[c])
 
-    tiles = 4
+    tiles = 2
     tile = product.shape[0] // tiles
 
     def multiply(c, start, stop):
@@ -679,7 +677,7 @@
     a_home = fa.at[dp, role]
     a_dp = {j: wires.send(a_home, a_home, dp_peer(j)) for j in range(1, dps)}
     a_role = {(0, k): wires.send(a_home, a_home, role_peer(k)) for k in near}
-    prompts_near(range(PARTS))
+    prompts_near([0, 1, 2])
     prompts_across([0])
     gather_forward(fb, b_role, b_dp, near[:1])
     for j in range(1, dps):
@@ -688,7 +686,7 @@
         for k in near:
             a_role[j, k] = wires.send(slot, slot, role_peer(k))
     gather_forward(fb, b_role, b_dp, near[1:])
-    loads["base"].start()
+    prompts_dp_landed([0])
     prompts_across([1])
     gather_finish(fb, b_dp)
     b_low = low_start(fb, cot, "cot", lb, rb)
@@ -697,23 +695,27 @@
         wires.landed(fa.at[dp_back(j), role_back(k)], place)
     a_low = low_start(fa, act, "act", la, ra)
     prompts_across([3])
-    prompts_dp_landed([0, 1])
+    prompts_hi_landed([0, 1, 2])
+    prompts_far_landed([0])
+    prompts_dp_landed([1])
+    prompts_near([3])
+    loads["own"].wait()
+    loads["base"].wait()
+    prompts_finish(0)
+    multiply(0, 0, 2)
 
     kept_grad = low_finish(lb, rb, b_low)
     xa_ids = reduce_start(pa, kept_grad, act, xa)
     kept_in = low_finish(la, ra, a_low)
     xb_ids = reduce_start(pb, kept_in, cot, xb)
     prompts_dp_landed([2])
-    prompts_hi_landed(range(PARTS))
-    prompts_far_landed([0])
+    prompts_far_landed([1])
     za_ids = reduce_middle(pa, xa, xa_ids, sa, za, oa, order)
     prompts_dp_landed([3])
-    loads["own"].wait()
-    loads["base"].wait()
-    prompts_finish(0)
-    multiply(0, 0, 4)
+    prompts_finish(1)
+    multiply(1, 0, 2)
     zb_ids = reduce_middle(pb, xb, xb_ids, sb, zb, ob, order[:2])
-    prompts_far_landed([1])
+    prompts_hi_landed([3])
 
     for name in ("am", "av", "bm", "bv"):
         loads[name].wait()
@@ -724,27 +726,33 @@
     mine = whole.at[tp]
     hi_ids, lo_a = {}, wires.take()
 
+    y_first = [0] + near[: roles // 2 - 1]
+    late_dp = {}
+
     def onward(j, k):
         slot = mine.at[dp_back(j), role_back(k)]
-        for h in range(1, half):
-            hi_ids[h, j, k] = wires.send(slot, slot, tp_peer(2 * h))
+        if j == 0 or k not in y_first:
+            for h in range(1, half):
+                hi_ids[h, j, k] = wires.send(slot, slot, tp_peer(2 * h))
         wires.send(slot, slot, lo_peer, lo_a)
 
     def beside(j, k):
         for h in range(1, half):
             slot = whole.at[tp_back(2 * h), dp_back(j), role_back(k)]
-            wires.landed(slot, hi_ids[h, j, k])
+            wires.landed(slot, late_dp[h, j, k] if j > 0 and k in y_first else hi_ids[h, j, k])
+            if j == 0 and k in y_first:
+                for other_j in range(1, dps):
+                    late_dp[h, other_j, k] = wires.send(slot, slot, dp_peer(other_j))
             wires.send(slot, slot, lo_peer, lo_a)
 
     a_role, a_dp = gather_start(mine)
     onward(0, 0)
     zb_ids.update(reduce_middle(pb, xb, xb_ids, sb, zb, ob, order[2:]))
     prompts_far_landed([2])
-    prompts_finish(1)
-    multiply(1, 0, 3)
+    prompts_finish(2)
+    multiply(2, 0, 2)
     gather_forward(mine, a_role, a_dp, near[:1])
     onward(0, near[0])
-    multiply(1, 3, 4)
     gather_forward(mine, a_role, a_dp, near[1:2])
     for k in near[1:2]:
         onward(0, k)
@@ -759,18 +767,19 @@
     for i in range(dps):
         b_send[i] = fresh[:, i * columns : (i + 1) * columns].astype(bf16)
     b_start()
-    prompts_finish(2)
-    for j in range(1, dps):
-        for k in [0] + near:
+    prompts_finish(3)
+    y_last = [k for k in near if k not in y_first]
+    for k in y_first + y_last:
+        if k in y_first:
+            beside(0, k)
+        for j in range(1, dps):
             wires.landed(mine.at[dp_back(j), role_back(k)], a_dp[j, k])
             onward(j, k)
-    multiply(2, 0, 4)
-    prompts_finish(3)
-    for k in [0] + near:
+    multiply(3, 0, 2)
+    for k in y_last:
         beside(0, k)
-    multiply(3, 0, 4)
-    for j in range(1, dps):
-        for k in [0] + near:
+    for k in y_first + y_last:
+        for j in range(1, dps):
             beside(j, k)
     wires.landed(whole.at[pl.ds(0, half)], lo_a)
     b_finish()
@@ -828,19 +837,20 @@
     saves = [pltpu.make_async_copy(x, y, small_sems.at[i]) for i, (x, y) in enumerate(zip(small, copies))]
     for save in saves:
         save.start()
-    depth, shards, tile, width = stage.shape
-    tiles = base.shape[0] // tile
+    depth, shards, groups, eight, width = stage.shape
+    tile = groups * eight
+    tiles = base.shape[0] // groups
 
     def out(i, shard):
-        rows = pl.ds(pl.multiple_of(i * tile, tile), tile)
+        rows = pl.ds(i * groups, groups)
         slot = lax.rem(i, depth)
-        target = merged_hbm.at[rows, shard * width : (shard + 1) * width]
+        target = merged_hbm.at[rows, :, shard * width : (shard + 1) * width]
         return pltpu.make_async_copy(stage.at[slot, shard], target, sems.at[slot, shard])
 
     @pl.loop(0, tiles)
     def _(i):
-        rows = pl.ds(pl.multiple_of(i * tile, tile), tile)
-        left = b[:, rows] * adapter_scale
+        rows = pl.ds(i * groups, groups)
+        left = b[:, pl.ds(pl.multiple_of(i * tile, tile), tile)] * adapter_scale
         for shard in range(shards):
 
             @pl.when(i >= depth)
@@ -848,8 +858,8 @@
                 out(i - depth, shard).wait()
 
         for shard in range(shards):
-            delta = contract_rows(left, a[shard])
-            merged = base[rows, shard * width : (shard + 1) * width].astype(jnp.float32) + delta
+            delta = contract_rows(left, a[shard]).reshape(groups, eight, width)
+            merged = base[rows, :, shard * width : (shard + 1) * width].astype(jnp.float32) + delta
             stage[lax.rem(i, depth), shard] = merged.astype(stage.dtype)
             out(i, shard).start()
 
@@ -860,7 +870,7 @@
     rest = (low - high.astype(jnp.float32)).astype(jnp.bfloat16)
 
     saved = []
-    for i in range(base.shape[0] // tile):
+    for i in range(tiles):
         rows = pl.ds(i * tile, tile)
         extra = contract_rows(b[:, rows], high) + contract_rows(b[:, rows], rest)
         projected[rows, :] = (product[rows, :] + adapter_scale * extra).astype(projected.dtype)
@@ -881,6 +891,7 @@
     count = prompts.shape[0]
     shards, _, part = a.shape
     vmem = pltpu.VMEM
+    base = base.reshape(rows // 8, 8, width)
     args = [pltpu.with_memory_space_constraint(x, pltpu.VMEM) for x in (*small, base, b, a, prompts, product)]
     return pl.pallas_call(
         finish_kernel,
@@ -889,7 +900,7 @@
         + [pltpu.HBM((rows, count), jnp.bfloat16)],
         in_specs=[VMEM] * len(args),
         out_specs=[HBM] * (len(small) + 2),
-        scratch_shapes=[vmem((2, shards, tile, part), base.dtype), vmem((rows, count), jnp.bfloat16), dma(2, shards), dma(1), dma(len(small))],
+        scratch_shapes=[vmem((2, shards, tile // 8, 8, part), base.dtype), vmem((rows, count), jnp.bfloat16), dma(2, shards), dma(1), dma(len(small))],
         compiler_params=pltpu.CompilerParams(vmem_limit_bytes=16 * 1024 * 1024),
         cost_estimate=pl.CostEstimate(
             flops=2 * rows * width * (count + b.shape[0]), bytes_accessed=4 * rows * width, transcendentals=0
@@ -916,6 +927,7 @@
         small,
     )
     a_new, a_mom, a_sec, b_new, b_mom, b_sec = copies
+    merged = merged.reshape(frozen_base_rows.shape)
     return a_new, b_new, a_mom, b_mom, a_sec, b_sec, merged, projected
 
 

time: 69 us -> 64.4 us (0.933)
  the two profiles are of different devices: /device:TPU:0 before, /device:TPU:3 now
where the time goes in v4:
time: 64.4 us; the launch traced here: 63.4 us
  Pallas kernels  62.1 us (96%)
  between operations  1.29 us (2%)
    pallas_call x1, Pallas kernels, step(): pl.pallas_call(step_kernel, name='step', out_shape=outs, in_specs=[HBM, H...  49.3 us
    pallas_call x1, Pallas kernels, finish(): pl.pallas_call(finish_kernel, name='finish', out_shape=[pltpu.HBM(x.shape...  12.8 us

profile of v4, /device:TPU:3, one launch (start us, length us, event | category | flops | bytes accessed | tf_op | source)
XLA Modules:
  0.0 63.4 jit_solution(1540781482523089181)
XLA Ops:
  1.3 49.3 %step.1 = (f32[8,2048]{1,0:T(8,128)S(1)}, f32[8,2048]{1,0:T(8,128)S(1)}, f32[8,2048]{1,0:T(8,128)S(1)}, f32[8,3584]{1,0:T(8,128)S(1)}, f32[8,3584]{1,0:T(8,128)S...) custom-call(bf16[256,2048]{1,0:T(8,128)(2,1)} %act_hbm.1, ...), custom_call_target="tpu_custom_call" | custom-call | flops 1000000000 | bytes 10000000 | tf_op jit(solution)/shard_map/step/pallas_call | solution.py:808
  50.5 12.8 %finish.1 = (f32[8,2048]{1,0:T(8,128)}, f32[8,2048]{1,0:T(8,128)}, f32[8,2048]{1,0:T(8,128)}, f32[8,3584]{1,0:T(8,128)}, f32[8,3584]{1,0:T(8,128)}, /*index=5*/f...) custom-call(f32[8,2048]{1,0:T(8,128)S(1)} %get-tuple-element.27.refs_0_, ...), custom_call_target="tpu_custom_call" | custom-call | flops 9395240960 | bytes 58720256 | tf_op jit(solution)/shard_map/finish/pallas_call | solution.py:896

commit v5 on v4

--- a/solution.py
+++ b/solution.py
@@ -699,10 +699,6 @@
     prompts_far_landed([0])
     prompts_dp_landed([1])
     prompts_near([3])
-    loads["own"].wait()
-    loads["base"].wait()
-    prompts_finish(0)
-    multiply(0, 0, 2)
 
     kept_grad = low_finish(lb, rb, b_low)
     xa_ids = reduce_start(pa, kept_grad, act, xa)
@@ -712,10 +708,13 @@
     prompts_far_landed([1])
     za_ids = reduce_middle(pa, xa, xa_ids, sa, za, oa, order)
     prompts_dp_landed([3])
-    prompts_finish(1)
-    multiply(1, 0, 2)
-    zb_ids = reduce_middle(pb, xb, xb_ids, sb, zb, ob, order[:2])
+    loads["own"].wait()
+    loads["base"].wait()
+    prompts_finish(0)
+    multiply(0, 0, 2)
+    zb_ids = reduce_middle(pb, xb, xb_ids, sb, zb, ob, order[:1])
     prompts_hi_landed([3])
+    prompts_far_landed([2])
 
     for name in ("am", "av", "bm", "bv"):
         loads[name].wait()
@@ -747,10 +746,9 @@
 
     a_role, a_dp = gather_start(mine)
     onward(0, 0)
-    zb_ids.update(reduce_middle(pb, xb, xb_ids, sb, zb, ob, order[2:]))
-    prompts_far_landed([2])
-    prompts_finish(2)
-    multiply(2, 0, 2)
+    zb_ids.update(reduce_middle(pb, xb, xb_ids, sb, zb, ob, order[1:]))
+    prompts_finish(1)
+    multiply(1, 0, 2)
     gather_forward(mine, a_role, a_dp, near[:1])
     onward(0, near[0])
     gather_forward(mine, a_role, a_dp, near[1:2])
@@ -767,7 +765,8 @@
     for i in range(dps):
         b_send[i] = fresh[:, i * columns : (i + 1) * columns].astype(bf16)
     b_start()
-    prompts_finish(3)
+    prompts_finish(2)
+    multiply(2, 0, 2)
     y_last = [k for k in near if k not in y_first]
     for k in y_first + y_last:
         if k in y_first:
@@ -775,6 +774,7 @@
         for j in range(1, dps):
             wires.landed(mine.at[dp_back(j), role_back(k)], a_dp[j, k])
             onward(j, k)
+    prompts_finish(3)
     multiply(3, 0, 2)
     for k in y_last:
         beside(0, k)

time: 64.4 us -> 63 us (0.978); the launches traced: 63.4 us -> 62.8 us
  no operation moved by 1% of the time
where the time goes in v5:
time: 63 us; the launch traced here: 62.8 us
  Pallas kernels  61.6 us (98%)
  between operations  1.29 us (2%)
    pallas_call x1, Pallas kernels, step(): pl.pallas_call(step_kernel, name='step', out_shape=outs, in_specs=[HBM, H...  48.7 us
    pallas_call x1, Pallas kernels, finish(): pl.pallas_call(finish_kernel, name='finish', out_shape=[pltpu.HBM(x.shape...  12.8 us

profile of v5, /device:TPU:3, one launch (start us, length us, event | category | flops | bytes accessed | tf_op | source)
XLA Modules:
  0.0 62.8 jit_solution(3916374970373962439)
XLA Ops:
  1.3 48.7 %step.1 = (f32[8,2048]{1,0:T(8,128)S(1)}, f32[8,2048]{1,0:T(8,128)S(1)}, f32[8,2048]{1,0:T(8,128)S(1)}, f32[8,3584]{1,0:T(8,128)S(1)}, f32[8,3584]{1,0:T(8,128)S...) custom-call(bf16[256,2048]{1,0:T(8,128)(2,1)} %act_hbm.1, ...), custom_call_target="tpu_custom_call" | custom-call | flops 1000000000 | bytes 10000000 | tf_op jit(solution)/shard_map/step/pallas_call | solution.py:808
  50.0 12.8 %finish.1 = (f32[8,2048]{1,0:T(8,128)}, f32[8,2048]{1,0:T(8,128)}, f32[8,2048]{1,0:T(8,128)}, f32[8,3584]{1,0:T(8,128)}, f32[8,3584]{1,0:T(8,128)}, /*index=5*/f...) custom-call(f32[8,2048]{1,0:T(8,128)S(1)} %get-tuple-element.27.refs_0_, ...), custom_call_target="tpu_custom_call" | custom-call | flops 9395240960 | bytes 58720256 | tf_op jit(solution)/shard_map/finish/pallas_call | solution.py:896
